TPU v7x, 256 devices: a 4x2x16 block of a 4x16x16 slice. The times are simulated.
256 devices in a mesh: runs: 2 (over y), amp: 128 (over z, x, core).
Axes of the slice: x: 4, y: 2, z: 16, core: 2. Of those that a mesh axis runs over, the one named last changes fastest.
The devices are a block of a 4x16x16 slice.
Arguments:
- initial_state: float32 [256, 1024, 128], P(('runs', 'amp')), parts along dimension 0, may hold values from -100 to 100
- gate_angles: float32 [10, 16], P('runs'), parts along dimension 0, may hold values from -3.140625 to 3.140625
- gate_pairs: int32 [5, 16, 2], replicated, may hold values from 0 to 6, as said below
- hop_coef: float32 [23], replicated, may hold values from 0.1 to 0.4
- hop_mask: int32 [23], replicated, may hold values 0 or 1
Outputs:
- adjoint: float32 [256, 1024, 128], P(('runs', 'amp')), parts along dimension 0
- block_grads: float32 [10, 128, 128], P('runs'), parts along dimension 0
There are 2 independent parts, one for each index of `runs`. A program takes and returns all parts, laid end to end along the dimension named above; an argument that names none is the same for every part. Nothing has to cross between parts.
Inputs may be any that keep to these rules, and one draw needn't show every extreme that they name: `gate_pairs`: the two qubits of each rotation differ.
All inputs are finite; a program needn't handle non-finite values.
Results may differ from a plain program's by a relative error of at most 0.0003.
Values sent between devices are 32-bit elements; how exact they have to be, the bound alone decides.
No kernel may reach another device: no remote copies, remote signals or barrier semaphores. Data moves between devices by JAX's collectives and lax.ppermute only.
A program may use at most 192 MiB of HBM per device.

v0:
```python
import jax
import jax.numpy as jnp
from jax import lax
from jax.sharding import Mesh
from jax.sharding import PartitionSpec as P

YQ = 3
AMP = ("amp_0", "amp_1", "amp_2")
RUNS_AMP = ("runs", "amp_0", "amp_1", "amp_2")


exact_mode = lax.Precision.HIGHEST
gram_forms = ["tci,tcj->ij", "tcia,tcja->ij", "abicd,abjcd->ij", "air,ajr->ij", "aicr,ajcr->ij"]
apply_forms = ["ij,tcj->tci", "ij,tcj->tci", "ij,abjcd->abicd", "ij,ajr->air", "ij,ajcr->aicr"]


def swapped(x, axis, bit):
    return lax.ppermute(x, axis, [(i, i ^ 1 << bit) for i in range(lax.axis_size(axis))])


def side_by_side(arrays, axis, split_dim, concat_dim, along):
    widths = [a.shape[along] for a in arrays]
    both = jnp.concatenate(arrays, axis=along)
    result = lax.all_to_all(both, axis, split_axis=split_dim, concat_axis=concat_dim, tiled=True)
    return tuple(jnp.split(result, [sum(widths[:k]) for k in range(1, len(widths))], axis=along))


def by_axis(x, axes):
    for axis in axes:
        x = lax.psum(x, axis)
    return x


def one_rotation(angle_now, pair_now, block_size):
    positions = jnp.arange(block_size, dtype=jnp.int32)
    diagonal = positions[:, None] == positions[None, :]
    one_bit = jnp.right_shift(positions, pair_now[0]) & 1
    two_bit = jnp.right_shift(positions, pair_now[1]) & 1
    flip_mask = jnp.left_shift(jnp.int32(1), pair_now[0]) | jnp.left_shift(
        jnp.int32(1), pair_now[1]
    )
    partner = jnp.bitwise_xor(positions, flip_mask)
    differ = (one_bit != two_bit)[:, None]
    zero_value = jnp.zeros((), angle_now.dtype)
    one_value = jnp.ones((), angle_now.dtype)
    sine_value = jnp.sin(angle_now)
    signed = jnp.where(one_bit < two_bit, -sine_value, sine_value)[:, None]
    rotation = jnp.where(diagonal, jnp.where(differ, jnp.cos(angle_now), one_value), zero_value)
    return rotation + jnp.where(
        differ & (positions[None, :] == partner[:, None]), signed, zero_value
    )


def build_blocks(gate_angles, gate_pairs, block_size):
    single = lambda angle_now, pair_now: one_rotation(angle_now, pair_now, block_size)
    factors = jax.vmap(jax.vmap(single))(gate_angles, gate_pairs)
    while factors.shape[1] > 1:
        factors = jnp.einsum(
            "bgij,bgjk->bgik", factors[:, 1::2], factors[:, 0::2], precision=exact_mode
        )
    return factors[:, 0]


def shaped_for(amplitudes, window):
    row_count, mid_count, lane_count = amplitudes.shape
    if window == 0:
        return amplitudes
    if window == 1:
        return amplitudes.reshape(row_count, mid_count // 4, lane_count, 4)
    if window == 2:
        stride = min(2 ** (YQ - 1), mid_count // lane_count)
        return amplitudes.reshape(
            row_count, mid_count // (stride * lane_count), lane_count, stride, lane_count
        )
    if window == 3:
        spread = lane_count // mid_count
        return amplitudes.reshape(row_count // spread, spread * mid_count, lane_count)
    return amplitudes.reshape(row_count // lane_count, lane_count, mid_count, lane_count)


def apply_local(amplitudes, unitary, window):
    row_count, mid_count, lane_count = amplitudes.shape
    if window == 1:
        widened = jnp.kron(unitary, jnp.eye(4, dtype=unitary.dtype))
        shaped = amplitudes.reshape(row_count, mid_count // 4, 4 * lane_count)
        return jnp.einsum(apply_forms[1], widened, shaped, precision=exact_mode).reshape(
            amplitudes.shape
        )
    shaped = shaped_for(amplitudes, window)
    return jnp.einsum(apply_forms[window], unitary, shaped, precision=exact_mode).reshape(
        amplitudes.shape
    )


def coupling_matrix(size, term_list, weights, dtype):
    positions = jnp.arange(size, dtype=jnp.int32)
    matrix = jnp.zeros((size, size), dtype)
    for lower, upper, slot in term_list:
        lower_bit = jnp.right_shift(positions, lower) & 1
        upper_bit = jnp.right_shift(positions, upper) & 1
        partner = jnp.bitwise_xor(positions, 1 << lower | 1 << upper)
        active = (lower_bit != upper_bit)[:, None] & (positions[None, :] == partner[:, None])
        matrix = matrix + jnp.where(active, weights[slot], jnp.zeros((), dtype))
    return matrix


def partner_half(amplitudes, local_bit, own_bit):
    flat_values = amplitudes.reshape(-1)
    total_size = flat_values.shape[0]
    shaped = flat_values.reshape(total_size // 2 ** (local_bit + 1), 2, 2**local_bit)
    return lax.dynamic_index_in_dim(shaped, 1 - own_bit, axis=1, keepdims=False)


def add_half(summed, received, scale, own_bit):
    full_shape = summed.shape
    shaped = summed.reshape(received.shape[0], 2, received.shape[1])
    present = lax.dynamic_index_in_dim(shaped, 1 - own_bit, axis=1, keepdims=True)
    updated = lax.dynamic_update_index_in_dim(
        shaped, present + scale * received[:, None, :], 1 - own_bit, axis=1
    )
    return updated.reshape(full_shape)


def hamiltonian_local(amplitudes, weights, my_index):
    row_count, mid_count, lane_count = amplitudes.shape
    full_shape = amplitudes.shape
    block_bits = lane_count.bit_length() - 1
    low_bits = mid_count.bit_length() - 1
    top_bits = row_count.bit_length() - 1
    pair_size = 2 * lane_count
    lane_terms = [(position, position + 1, position) for position in range(block_bits)]
    low_matrix = coupling_matrix(pair_size, lane_terms, weights, amplitudes.dtype)
    paired = amplitudes.reshape(row_count, mid_count // 2, pair_size)
    summed = jnp.einsum("ij,tcj->tci", low_matrix, paired, precision=exact_mode).reshape(full_shape)
    rung_base = block_bits + low_bits + top_bits - 1
    head_bits = 2 * low_bits
    head_terms = [(offset, offset + 1, block_bits + offset) for offset in range(low_bits - 1)]
    head_terms = head_terms + [
        (low_bits + offset, low_bits + offset + 1, block_bits + low_bits + offset)
        for offset in range(top_bits - 1)
        if low_bits + offset + 1 < head_bits
    ]
    head_terms = head_terms + [
        (offset, low_bits + offset, rung_base + offset) for offset in range(low_bits)
    ]
    head_matrix = coupling_matrix(2**head_bits, head_terms, weights, amplitudes.dtype)
    head_view = amplitudes.reshape(-1, 2**head_bits, lane_count)
    summed = summed + jnp.einsum(
        "ij,ajr->air", head_matrix, head_view, precision=exact_mode
    ).reshape(full_shape)
    tail_start = head_bits - 1
    tail_bits = low_bits + top_bits - tail_start
    tail_terms = [
        (
            low_bits + offset - tail_start,
            low_bits + offset + 1 - tail_start,
            block_bits + low_bits + offset,
        )
        for offset in range(top_bits - 1)
        if low_bits + offset + 1 >= head_bits
    ]
    tail_matrix = coupling_matrix(2**tail_bits, tail_terms, weights, amplitudes.dtype)
    tail_view = amplitudes.reshape(2**tail_bits, 2**tail_start, lane_count)
    summed = summed + jnp.einsum(
        "ij,jbr->ibr", tail_matrix, tail_view, precision=exact_mode
    ).reshape(full_shape)
    top_start = block_bits + low_bits
    own_first = my_index & 1
    chain_bit = block_bits + low_bits - 1
    rung_bit = top_start + low_bits
    chain_rows = partner_half(amplitudes, chain_bit, own_first)
    rung_rows = partner_half(amplitudes, rung_bit, own_first)
    chain_back, rung_back = swapped((chain_rows, rung_rows), AMP, 0)
    summed = add_half(summed, chain_back, weights[block_bits + low_bits - 1], own_first)
    summed = add_half(summed, rung_back, weights[rung_base + low_bits], own_first)
    for offset in range(1, top_bits - low_bits):
        own_bit = jnp.right_shift(my_index, offset) & 1
        far_bit = top_start + low_bits + offset
        half_rows = partner_half(amplitudes, far_bit, own_bit)
        returned = swapped(half_rows, AMP, offset)
        summed = add_half(summed, returned, weights[rung_base + low_bits + offset], own_bit)
    return summed


def on_device(initial_state, gate_angles, gate_pairs, hop_coef, hop_mask):
    lane_count = initial_state.shape[2]
    block_count = gate_angles.shape[0]
    my_index = lax.axis_index(AMP)
    weights = hop_coef * hop_mask.astype(hop_coef.dtype)
    block_stack = build_blocks(gate_angles, gate_pairs, lane_count)
    gate_blocks = [block_stack[number] for number in range(block_count)]
    factor = 2.0 / (initial_state.shape[0] * lax.axis_size(AMP) * initial_state.shape[1])
    layout = 0
    current = initial_state
    for number in range(block_count):
        window = number % 5
        wanted = 1 if window >= 3 else 0
        if wanted != layout:
            current = lax.all_to_all(current, AMP, split_axis=1, concat_axis=0, tiled=True)
            layout = wanted
        current = apply_local(current, gate_blocks[number], window)
    adjoint = hamiltonian_local(current, weights, my_index)
    collected = []
    for number in range(block_count - 1, block_count - 6, -1):
        window = number % 5
        wanted = 1 if window >= 3 else 0
        if wanted != layout:
            current, adjoint = side_by_side((current, adjoint), AMP, 0, 1, 2)
            layout = wanted
        transposed = gate_blocks[number].T
        current = apply_local(current, transposed, window)
        local_gram = jnp.einsum(
            gram_forms[window],
            shaped_for(adjoint, window),
            shaped_for(current, window),
            precision=exact_mode,
        )
        collected.append(factor * by_axis(local_gram, AMP))
        adjoint = apply_local(adjoint, transposed, window)
    block_grads = jnp.stack(collected[::-1])
    return (adjoint, block_grads)


def solution(mesh):
    split = Mesh(
        mesh.devices.reshape(mesh.shape["runs"], 16, 4, 2), ("runs", "amp_0", "amp_1", "amp_2")
    )
    return jax.shard_map(
        on_device,
        mesh=split,
        in_specs=(P(RUNS_AMP, None, None), P("runs", None), P(), P(), P()),
        out_specs=(P(RUNS_AMP, None, None), P("runs", None, None)),
        check_vma=False,
    )
```

profile of v0, /device:TPU:33, one launch (start us, length us, event | category | flops | bytes accessed | tf_op | source)
XLA Modules:
  0.0 522.9 jit_solution(7746222785642798933)
XLA Ops:
  9.1 5.6 %select_add_fusion = f32[5,16,128,128]{3,2,1,0:T(8,128)S(1)} fusion(f32[5,16,128]{2,1,0:T(8,128)S(1)} %get-tuple-element.22, s32[5,16,128]{2,1,0:T(8,128)S(1)} %iota_xor_fusion, f32[5,16,128]{2,1,0:T(8,128)S(1)} %get-tuple-element.21, pred[5,16,128]{2,1,0:T(8,128)(4,1)S(1)} %fusion.95, pred[128,128]{1,0:T(8,128)(4,1)S(1)} %iota_compare_fusion.8), kind=kLoop, calls=%fused_computation.2 | loop fusion | flops 6553600 | bytes 5392384 | tf_op jit(solution)/shard_map/vmap(vmap())/add | solution.py:49
  14.6 3.1 fusion.1
  17.8 1.5 fusion.4
  20.6 22.0 %broadcast_multiply_fusion.1 = (f32[128,4,128,4]{3,2,1,0:T(8,128)}, f32[128,4,128,4]{3,2,1,0:T(8,128)}) fusion(f32[4,4]{1,0:T(4,128)S(1)} %fusion.178, f32[128,128]{1,0:T(8,128)S(1)} %get-tuple-element.19, f32[128,128]{1,0:T(8,128)S(1)} %copy.130), kind=kLoop, calls=%fused_computation.1 | loop fusion | flops 524288 | bytes 2228288 | tf_op jit(solution)/shard_map/jit(kron)/mul | solution.py:84
  42.6 29.0 %reshape.446 = f32[4,128,512,1]{2,1,0,3:T(8,128)S(1)} reshape(f32[128,4,128,4]{3,2,1,0:T(8,128)} %get-tuple-element.30) | data formatting | bytes 2097152 | tf_op jit(solution)/shard_map/jit(kron)/mul | solution.py:84
  75.3 31.0 %all-to-all-start = ((f32[1,1024,128]{2,0,1:T(1,128)}), f32[1,1024,128]{2,0,1:T(1,128)S(1)}, u32[]{:S(2)}, u32[]{:S(2)}) async-start(f32[1,1024,128]{2,0,1:T(1,128)} %bitcast.16), calls=%async_computation | async-start | bytes 1048576 | tf_op jit(solution)/shard_map/all_to_all | solution.py:199
  108.0 29.1 %all-to-all-done = f32[1,1024,128]{2,0,1:T(1,128)S(1)} async-done(((f32[1,1024,128]{2,0,1:T(1,128)}), f32[1,1024,128]{2,0,1:T(1,128)S(1)}, u32[]{:S(2)}, u32[]{:S(2)}) %all-to-all-start) | async-done | bytes 524320 | tf_op jit(solution)/shard_map/all_to_all | solution.py:199
  142.6 3.4 fusion.29
  146.8 5.3 %convolution_bitcast_fusion.3 = f32[16,64,128]{2,1,0:T(8,128)S(1)} fusion(f32[16,64,128]{2,1,0:T(8,128)S(1)} %bitcast.238, f32[]{:T(128)} %bitcast.52, s32[64]{0:T(128)S(1)} %get-tuple-element.65, f32[]{:T(128)} %bitcast.51, s32[64]{0:T(128)S(1)} %get-tuple-element.66, f32[]{:T(128)} %bitcast.50, s32[64]{0:T(128)S(1)} %get-tuple-element.67, f32[]{:T(128)} %bitcast.49, ...), kind=kOutput, calls=%fused_computation.14 | convolution fusion | flops 100773888 | bytes 1050844 | tf_op jit(solution)/shard_map/ij,ajr->air/dot_general | solution.py:148
  153.3 1.3 constant_dynamic-slice_fusion.2
  157.7 1.9 collective-permute-start.2
  160.7 2.9 collective-permute-start.3
  164.5 10.4 %collective-permute-start.4 = (f32[1,65536]{1,0:T(1,128)}, f32[1,65536]{1,0:T(1,128)}, u32[]{:S(2)}, u32[]{:S(2)}) collective-permute-start(f32[1,65536]{1,0:T(1,128)} %dynamic-slice_bitcast_fusion), channel_id=1, source_target_pairs={{0,8},{1,9},{2,10},{3,11},{4,12},{5,13},{6,14},{7,15},{8,0},{9,1},... | collective-permute-start | bytes 786440 | tf_op jit(solution)/shard_map/ppermute | solution.py:18
  175.0 5.4 %fusion.39 = f32[128,4,256]{0,2,1:T(8,128)S(1)} fusion(f32[128,4,256]{0,2,1:T(8,128)S(1)} %bitcast.241, f32[]{:T(128)} %bitcast.42, s32[256]{0:T(256)S(1)} %get-tuple-element.77, f32[]{:T(128)} %bitcast.41, s32[256]{0:T(256)S(1)} %get-tuple-element.78, f32[]{:T(128)} %bitcast.40, s32[256]{0:T(256)S(1)} %get-tuple-element.81, f32[]{:T(128)} %bitcast.39, ...), kind=kOutput, calls=%fused_computation.62 | convolution fusion | flops 404422656 | bytes 1057564 | tf_op jit(solution)/shard_map/ij,tcj->tci/dot_general | solution.py:134
  183.5 1.6 broadcast_multiply_fusion.4
  185.5 2.8 dynamic_update_slice.21
  188.9 1.6 broadcast_multiply_fusion.3
  190.9 3.3 dynamic_update_slice.22
  194.8 1.7 broadcast_multiply_fusion.2
  196.8 3.3 dynamic_update_slice.23
  200.8 2.0 bitcast_add_fusion.1
  202.8 3.3 dynamic_update_slice.24
  209.2 9.2 %all-to-all-start.1 = ((f32[128,8,256]{2,1,0:T(8,128)}), f32[128,8,256]{2,1,0:T(8,128)}, u32[]{:S(2)}, u32[]{:S(2)}) async-start(f32[128,8,256]{2,1,0:T(8,128)} %pad_maximum_fusion), calls=%async_computation.1 | async-start | bytes 2097152 | tf_op jit(solution)/shard_map/all_to_all | solution.py:24
  218.7 28.7 %mul.169 = f32[512,512]{1,0:T(8,128)S(1)} reshape(f32[128,4,128,4]{3,2,1,0:T(8,128)} %get-tuple-element.31) | data formatting | bytes 2097152 | tf_op jit(solution)/shard_map/jit(kron)/mul | solution.py:84
  249.8 19.6 %all-to-all-done.1 = f32[128,8,256]{2,1,0:T(8,128)} async-done(((f32[128,8,256]{2,1,0:T(8,128)}), f32[128,8,256]{2,1,0:T(8,128)}, u32[]{:S(2)}, u32[]{:S(2)}) %all-to-all-start.1) | async-done | bytes 1048608 | tf_op jit(solution)/shard_map/all_to_all | solution.py:24
  278.4 1.6 fusion.90
  280.0 1.9 fusion.13
  284.3 1.6 fusion.211
  286.0 119.5 %all-reduce.7.cloned.1.call-done = (f32[128,128]{1,0:T(8,128)}, f32[128,128]{1,0:T(8,128)}, f32[128,128]{1,0:T(8,128)}, f32[128,128]{1,0:T(8,128)}, f32[128,128]{1,0:T(8,128)}) async-done(((f32[128,128]{1,0:T(8,128)}, f32[128,128]{1,0:T(8,128)}, f32[128,128]{1,0:T(8,128)}, f32[128,128]{1,0:T(8,128)}, f32[128,128]{1,0:T(8,128)}), (f32[128,128]{1,0:T(8,128)}, f32[128,128]{1,0:T(8,128)}, f32[128,128]{1,0:T(8,128)}, ...) | async-done | bytes 327696 | tf_op jit(solution)/shard_map/psum | solution.py:30
  405.6 61.8 %all-reduce.9.cloned.1.call-done = (f32[128,128]{1,0:T(8,128)}, f32[128,128]{1,0:T(8,128)}, f32[128,128]{1,0:T(8,128)}, f32[128,128]{1,0:T(8,128)}, f32[128,128]{1,0:T(8,128)}) async-done(((f32[128,128]{1,0:T(8,128)}, f32[128,128]{1,0:T(8,128)}, f32[128,128]{1,0:T(8,128)}, f32[128,128]{1,0:T(8,128)}, f32[128,128]{1,0:T(8,128)}), (f32[128,128]{1,0:T(8,128)}, f32[128,128]{1,0:T(8,128)}, f32[128,128]{1,0:T(8,128)}, ...) | async-done | bytes 327696 | tf_op jit(solution)/shard_map/psum | solution.py:30
  467.5 1.4 convolution_bitcast_fusion
  468.9 42.2 %all-reduce.11.cloned.1.call-done = (f32[128,128]{1,0:T(8,128)}, f32[128,128]{1,0:T(8,128)}, f32[128,128]{1,0:T(8,128)}, f32[128,128]{1,0:T(8,128)}, f32[128,128]{1,0:T(8,128)}) async-done(((f32[128,128]{1,0:T(8,128)}, f32[128,128]{1,0:T(8,128)}, f32[128,128]{1,0:T(8,128)}, f32[128,128]{1,0:T(8,128)}, f32[128,128]{1,0:T(8,128)}), (f32[128,128]{1,0:T(8,128)}, f32[128,128]{1,0:T(8,128)}, ...) | async-done | bytes 327696 | tf_op jit(solution)/shard_map/psum | solution.py:30
  (127 shorter events, 49.3 us)
Async XLA Ops:
  7.2 64.4 %copy-start = (f32[1,1024,128]{2,1,0:T(8,128)S(1)}, f32[1,1024,128]{2,1,0:T(8,128)}, u32[]{:S(2)}) copy-start(f32[1,1024,128]{2,1,0:T(8,128)} %param.5) | copy-start | bytes 1572868
  72.5 34.1 %copy-start.5 = (f32[23]{0:T(128)S(1)}, f32[23]{0:T(128)}, u32[]{:S(2)}) copy-start(f32[23]{0:T(128)} %param.8) | copy-start | bytes 280
  72.5 34.1 %copy-start.6 = (s32[23]{0:T(128)S(1)}, s32[23]{0:T(128)}, u32[]{:S(2)}) copy-start(s32[23]{0:T(128)} %param.9) | copy-start | bytes 280
  75.3 61.7 %all-to-all-start = ((f32[1,1024,128]{2,0,1:T(1,128)}), f32[1,1024,128]{2,0,1:T(1,128)S(1)}, u32[]{:S(2)}, u32[]{:S(2)}) async-start(f32[1,1024,128]{2,0,1:T(1,128)} %bitcast.16), calls=%async_computation | async-start | bytes 1048576 | tf_op jit(solution)/shard_map/all_to_all | solution.py:199
  152.4 7.2 %copy-start.3 = (f32[2,2,32768]{2,1,0:T(2,128)S(1)}, f32[2,2,32768]{2,1,0:T(2,128)}, u32[]{:S(2)}) copy-start(f32[2,2,32768]{2,1,0:T(2,128)} %reshape_reshape_reshape.18) | copy-start | bytes 1572868
  152.7 29.4 %collective-permute-start = (f32[128,512]{0,1:T(8,128)S(1)}, f32[128,512]{0,1:T(8,128)S(1)}, u32[]{:S(2)}, u32[]{:S(2)}) collective-permute-start(f32[128,512]{0,1:T(8,128)S(1)} %dynamic-slice_bitcast_fusion.1), channel_id=1, source_target_pairs={{0,1},{1,0},{2,3},{3,2},{4,5},{5,4},{6,7},{7,6},{8,9},{9,8},{10,11... | collective-permute-start | bytes 786440 | tf_op jit(solution)/shard_map/ppermute | solution.py:18
  155.4 28.1 %collective-permute-start.1 = (f32[8,8192]{1,0:T(8,128)}, f32[8,8192]{1,0:T(8,128)}, u32[]{:S(2)}, u32[]{:S(2)}) collective-permute-start(f32[8,8192]{1,0:T(8,128)} %bitcast.235), channel_id=1, source_target_pairs={{0,1},{1,0},{2,3},{3,2},{4,5},{5,4},{6,7},{7,6},{8,9},{9,8},{10,11... | collective-permute-start | bytes 786440 | tf_op jit(solution)/shard_map/ppermute | solution.py:18
  157.7 31.3 %collective-permute-start.2 = (f32[4,16384]{1,0:T(4,128)}, f32[4,16384]{1,0:T(4,128)}, u32[]{:S(2)}, u32[]{:S(2)}) collective-permute-start(f32[4,16384]{1,0:T(4,128)} %bitcast.234), channel_id=1, source_target_pairs={{0,2},{1,3},{2,0},{3,1},{4,6},{5,7},{6,4},{7,5},{8,10},{9,11},{10,... | collective-permute-start | bytes 786440 | tf_op jit(solution)/shard_map/ppermute | solution.py:18
  160.7 34.1 %collective-permute-start.3 = (f32[2,32768]{1,0:T(2,128)}, f32[2,32768]{1,0:T(2,128)}, u32[]{:S(2)}, u32[]{:S(2)}) collective-permute-start(f32[2,32768]{1,0:T(2,128)} %bitcast.233), channel_id=1, source_target_pairs={{0,4},{1,5},{2,6},{3,7},{4,0},{5,1},{6,2},{7,3},{8,12},{9,13},{10,... | collective-permute-start | bytes 786440 | tf_op jit(solution)/shard_map/ppermute | solution.py:18
  164.5 36.3 %collective-permute-start.4 = (f32[1,65536]{1,0:T(1,128)}, f32[1,65536]{1,0:T(1,128)}, u32[]{:S(2)}, u32[]{:S(2)}) collective-permute-start(f32[1,65536]{1,0:T(1,128)} %dynamic-slice_bitcast_fusion), channel_id=1, source_target_pairs={{0,8},{1,9},{2,10},{3,11},{4,12},{5,13},{6,14},{7,15},{8,0},{9,1},... | collective-permute-start | bytes 786440 | tf_op jit(solution)/shard_map/ppermute | solution.py:18
  209.2 60.2 %all-to-all-start.1 = ((f32[128,8,256]{2,1,0:T(8,128)}), f32[128,8,256]{2,1,0:T(8,128)}, u32[]{:S(2)}, u32[]{:S(2)}) async-start(f32[128,8,256]{2,1,0:T(8,128)} %pad_maximum_fusion), calls=%async_computation.1 | async-start | bytes 2097152 | tf_op jit(solution)/shard_map/all_to_all | solution.py:24
  218.4 187.1 %all-reduce.7.cloned.1.call-start = ((), (), s32[]{:S(2)}) async-start(), calls=%async_computation.2 | async-start | bytes 655360 | tf_op jit(solution)/shard_map/psum | solution.py:30
  277.7 2.3 copy-start.2
  281.8 234.2 %copy-start.1 = (f32[1,1024,128]{2,1,0:T(8,128)S(1)}, f32[1,1024,128]{2,1,0:T(8,128)}, u32[]{:S(2)}) copy-start(f32[1,1024,128]{2,1,0:T(8,128)} %param.5) | copy-start | bytes 1572868
  286.0 181.5 %all-reduce.9.cloned.1.call-start = ((), (), s32[]{:S(2)}) async-start(), calls=%async_computation.3 | async-start | bytes 655360 | tf_op jit(solution)/shard_map/psum | solution.py:30
  405.6 105.5 %all-reduce.11.cloned.1.call-start = ((), (), s32[]{:S(2)}) async-start(), calls=%async_computation.4 | async-start | bytes 655360 | tf_op jit(solution)/shard_map/psum | solution.py:30
  515.3 0.7 copy-start.4
Sparse Core Ops, SparseCore 0:
  286.1 119.3 all-reduce.6
  408.2 59.2 all-reduce.8
  470.4 40.5 all-reduce.10
where the time goes:
time: 532 us; the launch traced here: 523 us
  waiting for transfers between devices  272 us (51%)
  local copies, waits for them, and re-layouts  96.7 us (18%)
  starting transfers between devices  56.5 us (11%)
  other arithmetic  41.8 us (8%)
  matrix products  40.7 us (8%)
  between operations  14.9 us (3%)
    psum x3, waiting for transfers between devices, by_axis(): x = lax.psum(x, axis)  223 us
    mul x3, local copies, waits for them, and re-layouts, apply_local(): widened = jnp.kron(unitary, jnp.eye(4, dtype=unitary.dtype))  57.7 us
    all_to_all x1, starting transfers between devices, on_device(): lax.all_to_all(current, AMP, split_axis=1, concat_axis=0, tiled=True)  31 us
    all_to_all x1, waiting for transfers between devices, on_device(): lax.all_to_all(current, AMP, split_axis=1, concat_axis=0, tiled=True)  29.1 us
    mul x1, other arithmetic, apply_local(): widened = jnp.kron(unitary, jnp.eye(4, dtype=unitary.dtype))  22 us
    all_to_all x1, waiting for transfers between devices, side_by_side(): lax.all_to_all(both, axis, split_axis=split_dim, concat_axis=concat_dim,...  19.6 us
    ppermute x5, starting transfers between devices, swapped(): lax.ppermute(x, axis, [(i, i ^ 1 << bit) for i in range(lax.axis_size(axi...  15.9 us
    dynamic_update_slice x5, local copies, waits for them, and re-layouts, add_half(): lax.dynamic_update_index_in_dim(shaped, present + scale * received[:, Non...  12.9 us
  transfers between devices with their start and end apart: 10, of which 5 were waited for; matrix products, arithmetic and copies ran while one was open for 13% of the time, Pallas kernels for 0%

commit v1 on v0

v1 whole, which is shorter than its diff:
```python
import functools

import jax
import jax.numpy as jnp
from jax import lax
from jax.experimental import pallas as pl
from jax.experimental.pallas import tpu as pltpu
from jax.sharding import PartitionSpec as P

F32, BF16 = jnp.float32, jnp.bfloat16
AMP = "amp"
VMEM = pl.BlockSpec(memory_space=pltpu.VMEM)
SMEM = pl.BlockSpec(memory_space=pltpu.SMEM)

LANES = 128
LOW = 8
PARTS = 4
PACK = LOW + 2
CHAIN_FIRST = 10
RUNG_FIRST = 16


def chunk_of(device):
    return device ^ (((device >> 2) & 1) << 1)


def halves(value):
    high = value.astype(BF16)
    return high, (value - high.astype(F32)).astype(BF16)


def product(left, right, left_dim, right_dim):
    dims = (((left_dim,), (right_dim,)), ((), ()))
    dot = lambda a, b: lax.dot_general(a, b, dims, preferred_element_type=F32)
    return dot(left[0], right[0]) + (dot(left[0], right[1]) + dot(left[1], right[0]))


def own_bits():
    chunk = chunk_of(lax.axis_index(AMP))
    return [(chunk >> k) & 1 for k in range(4)]


def spread_selector():
    rows = lax.broadcasted_iota(jnp.int32, (PARTS * LANES, LANES), 0)
    columns = lax.broadcasted_iota(jnp.int32, (PARTS * LANES, LANES), 1)
    return ((rows >> 2) == columns).astype(F32).astype(BF16)


def same_part():
    shape = (PARTS * LANES, PARTS * LANES)
    rows = lax.broadcasted_iota(jnp.int32, shape, 0)
    columns = lax.broadcasted_iota(jnp.int32, shape, 1)
    return ((rows ^ columns) & (PARTS - 1)) == 0


def forward_kernel(angles, pairs, x, send, s1, s2, gates, k_high, k_low, cosines, sines, nat):
    block_count, rotation_count = angles.shape
    cosines[...] = jnp.cos(angles[...])
    sines[...] = jnp.sin(angles[...])
    row = lax.broadcasted_iota(jnp.int32, (LANES, LANES), 0)
    apart = row ^ lax.broadcasted_iota(jnp.int32, (LANES, LANES), 1)

    def build(b, carry):
        cos_row = cosines[pl.ds(b, 1), :]
        sin_row = sines[pl.ds(b, 1), :]

        def rotation(g):
            first = pairs[b * (2 * rotation_count) + 2 * g]
            second = pairs[b * (2 * rotation_count) + 2 * g + 1]
            flip = (1 << first) | (1 << second)
            one = (row >> first) & 1
            differ = one != ((row >> second) & 1)
            sine = sin_row[:, g : g + 1]
            off = jnp.where(one == 1, sine, -sine)
            value = jnp.where(differ & (apart == flip), off, 0.0)
            return jnp.where(apart == 0, jnp.where(differ, cos_row[:, g : g + 1], 1.0), value)

        def chain(low, count):
            if count == 1:
                return rotation(low)
            half = count // 2
            first = chain(low, half)
            return product(halves(chain(low + half, half)), halves(first), 1, 0)

        gates[b] = chain(0, rotation_count)
        return carry

    lax.fori_loop(0, block_count, build, 0)

    g0 = halves(gates[0])
    for q in range(PARTS):
        part = x[pl.ds(q, x.shape[0] // PARTS, stride=PARTS), :]
        s1[:, q * LANES : (q + 1) * LANES] = product(halves(part), g0, 1, 1)
    g1 = halves(gates[1])
    pick = spread_selector()
    keep = same_part()
    for out, source in ((k_high, g1[0]), (k_low, g1[1])):
        tall = jnp.dot(pick, source, preferred_element_type=F32).astype(BF16)
        wide = lax.dot_general(tall, pick, (((1,), (1,)), ((), ())), preferred_element_type=F32)
        out[...] = jnp.where(keep, wide, 0.0).astype(BF16)
    s2[...] = product(halves(s1[...]), (k_high[...], k_low[...]), 1, 1)
    g2 = halves(gates[2])
    for e in range(s2.shape[0] // LANES):
        s3 = product(g2, halves(s2[e * LANES : (e + 1) * LANES, :]), 1, 0)
        for q in range(PARTS):
            nat[pl.ds(e * PARTS * LANES + q, LANES, stride=PARTS), :] = s3[:, q * LANES : (q + 1) * LANES]
    for d in range(send.shape[0] // LOW):
        c = chunk_of(d)
        send[d * LOW : (d + 1) * LOW, :] = nat[c * LOW : (c + 1) * LOW, :]


def turn_kernel(z, gates, v, u4, half4, half5, half6, scratch):
    bits = own_bits()
    g3 = halves(gates[3])
    for block in range(z.shape[0] // LANES):
        rows = slice(block * LANES, (block + 1) * LANES)
        scratch[rows, :] = product(g3, halves(z[rows, :]), 1, 0)
    for c in range(LOW):
        u4[:, c * LANES : (c + 1) * LANES] = scratch[pl.ds(c, LANES, stride=LOW), :]
    v[...] = product(halves(gates[4]), halves(u4[...]), 1, 0)
    for out, k in ((half4, 4), (half5, 5), (half6, 6)):
        size = 1 << k
        for j in range(LANES // (2 * size)):
            start = pl.multiple_of(j * 2 * size + (1 - bits[k - 3]) * size, size)
            out[j * size : (j + 1) * size, :] = v[pl.ds(start, size), :]


def weight(coef, mask, number):
    return coef[number] * mask[number].astype(F32)


def pair_matrix(low, high, scale):
    rows = lax.broadcasted_iota(jnp.int32, (LANES, LANES), 0)
    columns = lax.broadcasted_iota(jnp.int32, (LANES, LANES), 1)
    active = (((rows >> low) ^ (rows >> high)) & 1) == 1
    return jnp.where(active & ((rows ^ columns) == ((1 << low) | (1 << high))), scale, 0.0)


def local_hops_kernel(v, coef, mask, out):
    lane_chain = sum(pair_matrix(k, k + 1, weight(coef, mask, k)) for k in range(6))
    top_chain = sum(pair_matrix(k, k + 1, weight(coef, mask, CHAIN_FIRST + k)) for k in range(6))
    lane_chain, top_chain = halves(lane_chain), halves(top_chain)
    rows = lax.broadcasted_iota(jnp.int32, (LANES, LANES), 0)
    columns = lax.broadcasted_iota(jnp.int32, (LANES, LANES), 1)
    rungs = []
    for k in range(3):
        scale = weight(coef, mask, RUNG_FIRST + k)
        paired = (rows ^ columns) == (1 << k)
        rungs.append([halves(jnp.where(paired & (((rows >> k) & 1) == 1 - c), scale, 0.0)) for c in range(2)])
    blocks = [v[:, c * LANES : (c + 1) * LANES] for c in range(LOW)]
    parts = [halves(block) for block in blocks]
    for c in range(LOW):
        total = product(parts[c], lane_chain, 1, 0) + product(top_chain, parts[c], 1, 0)
        for k in range(3):
            total = total + product(rungs[k][(c >> k) & 1], parts[c ^ (1 << k)], 1, 0)
        moved = pltpu.roll(blocks[c ^ 1], LANES // 2, 1)
        wanted = (columns >> 6) == 1 - (c & 1)
        total = total + jnp.where(wanted, weight(coef, mask, 6) * moved, 0.0)
        for k in range(2):
            if (c >> k) & 1 != (c >> (k + 1)) & 1:
                total = total + weight(coef, mask, 7 + k) * blocks[c ^ (3 << k)]
        out[:, c * LANES : (c + 1) * LANES] = total


def return_kernel(hops, other, half4, half5, half6, coef, mask, u4, z, gates, send, lam, scratch):
    bits = own_bits()
    lam[...] = hops[...]
    wide = lam.shape[1] // 2
    to = pl.multiple_of((1 - bits[0]) * wide, wide)
    source = pl.multiple_of(bits[0] * wide, wide)
    lam[:, pl.ds(to, wide)] += weight(coef, mask, 9) * other[:, pl.ds(source, wide)]
    for j in range(LANES // 16):
        to = pl.multiple_of(j * 16 + (1 - bits[0]) * 8, 8)
        source = pl.multiple_of(j * 16 + bits[0] * 8, 8)
        lam[pl.ds(to, 8), :] += weight(coef, mask, RUNG_FIRST + 3) * other[pl.ds(source, 8), :]
    for half, k in ((half4, 4), (half5, 5), (half6, 6)):
        size = 1 << k
        for j in range(LANES // (2 * size)):
            to = pl.multiple_of(j * 2 * size + (1 - bits[k - 3]) * size, size)
            lam[pl.ds(to, size), :] += weight(coef, mask, RUNG_FIRST + k) * half[j * size : (j + 1) * size, :]
    lam5 = halves(lam[...])
    top_rows = send.shape[0] // PACK
    send[pl.ds(LOW, top_rows, stride=PACK), :] = product(lam5, halves(u4[...]), 1, 1)
    lam4 = product(halves(gates[4]), lam5, 0, 0)
    for c in range(LOW):
        scratch[pl.ds(c, LANES, stride=LOW), :] = lam4[:, c * LANES : (c + 1) * LANES]
    g3 = halves(gates[3])
    gram = jnp.zeros((LANES, LANES), F32)
    for block in range(z.shape[0] // LANES):
        rows = slice(block * LANES, (block + 1) * LANES)
        inner = halves(scratch[rows, :])
        gram = gram + product(inner, halves(z[rows, :]), 1, 1)
        lam3 = product(g3, inner, 0, 0)
        for t in range(LANES // LOW):
            start = (block * (LANES // LOW) + t) * PACK
            send[start : start + LOW, :] = lam3[t * LOW : (t + 1) * LOW, :]
    send[pl.ds(LOW + 1, top_rows, stride=PACK), :] = gram


def backward_kernel(received, x, s1, s2, gates, k_high, k_low, adjoint, pack, nat):
    sources = received.shape[0] // PACK
    for d in range(sources):
        c = chunk_of(d)
        nat[c * LOW : (c + 1) * LOW, :] = received[d * PACK : d * PACK + LOW, :]
    for k in range(2):
        mine = jnp.sum(received[pl.ds(LOW + k, sources, stride=PACK), :], axis=0, keepdims=True)
        pack[pl.ds(3 + k, sources, stride=5), :] = jnp.broadcast_to(mine, (sources, LANES))
    count = x.shape[0] // PARTS
    g2 = halves(gates[2])
    gram2 = jnp.zeros((LANES, LANES), F32)
    pieces = []
    for e in range(count // LANES):
        lam3 = jnp.concatenate(
            [nat[pl.ds(e * PARTS * LANES + q, LANES, stride=PARTS), :] for q in range(PARTS)], axis=1
        )
        lam3 = halves(lam3)
        gram2 = gram2 + product(lam3, halves(s2[e * LANES : (e + 1) * LANES, :]), 1, 1)
        pieces.append(product(g2, lam3, 0, 0))
    lam2 = halves(jnp.concatenate(pieces, axis=0))
    wide = jnp.where(same_part(), product(lam2, halves(s1[...]), 0, 0), 0.0)
    pick = spread_selector()
    dims = (((0,), (0,)), ((), ()))
    high, low = halves(wide)
    dot = functools.partial(lax.dot_general, preferred_element_type=F32)
    folded = dot(pick, high, dims) + dot(pick, low, dims)
    high, low = halves(folded)
    gram1 = jnp.dot(high, pick, preferred_element_type=F32) + jnp.dot(low, pick, preferred_element_type=F32)
    lam1 = product(lam2, (k_high[...], k_low[...]), 1, 0)
    g0 = halves(gates[0])
    gram0 = jnp.zeros((LANES, LANES), F32)
    for q in range(PARTS):
        inner = halves(lam1[:, q * LANES : (q + 1) * LANES])
        gram0 = gram0 + product(inner, halves(x[pl.ds(q, count, stride=PARTS), :]), 0, 0)
        adjoint[pl.ds(q, count, stride=PARTS), :] = product(inner, g0, 1, 0)
    for k, gram in enumerate((gram0, gram1, gram2)):
        pack[pl.ds(k, sources, stride=5), :] = gram


def reduce_kernel(received, grads, pack, *, factor):
    sources = received.shape[0] // 5
    for k in range(3):
        mine = jnp.sum(received[pl.ds(k, sources, stride=5), :], axis=0, keepdims=True)
        pack[pl.ds(k, sources, stride=3), :] = jnp.broadcast_to(factor * mine, (sources, LANES))
    grads[0] = factor * received[pl.ds(4, sources, stride=5), :]
    grads[1] = factor * received[pl.ds(3, sources, stride=5), :]


def gather_kernel(received, upper, grads):
    sources = received.shape[0] // 3
    for k in range(3):
        grads[k] = received[pl.ds(k, sources, stride=3), :]
    for k in range(2):
        grads[3 + k] = upper[k]


def call(kernel, outs, specs, scratch=(), name=None):
    return pl.pallas_call(
        kernel,
        out_shape=[jax.ShapeDtypeStruct(shape, dtype) for shape, dtype in outs],
        in_specs=specs,
        out_specs=[VMEM] * len(outs),
        scratch_shapes=list(scratch),
        name=name,
    )


def exchange(rows):
    devices = lax.axis_size(AMP)
    shaped = rows.reshape(devices, rows.shape[0] // devices, 1, rows.shape[1])
    return lax.all_to_all(shaped, AMP, split_axis=0, concat_axis=0, tiled=True).reshape(rows.shape)


def swapped(value, flip):
    return lax.ppermute(value, AMP, [(i, i ^ flip) for i in range(lax.axis_size(AMP))])


def on_device(initial_state, gate_angles, gate_pairs, hop_coef, hop_mask):
    devices = lax.axis_size(AMP)
    middle = initial_state.shape[1]
    x = initial_state.reshape(middle, LANES)
    blocks = gate_angles.shape[0]
    wide = (middle // PARTS, PARTS * LANES)
    turned = (devices, LOW * LANES)
    square = (PARTS * LANES, PARTS * LANES)
    table = pltpu.VMEM(gate_angles.shape, F32)
    flat = pltpu.VMEM((middle, LANES), F32)

    send, s1, s2, gates, k_high, k_low = call(
        forward_kernel,
        [((middle, LANES), F32), (wide, F32), (wide, F32), ((blocks, LANES, LANES), F32), (square, BF16), (square, BF16)],
        [VMEM, SMEM, VMEM],
        [table, table, flat],
        "forward",
    )(gate_angles, gate_pairs.reshape(-1), x)
    z = exchange(send)
    half = (devices // 2, LOW * LANES)
    v, u4, half4, half5, half6 = call(
        turn_kernel,
        [(turned, F32), (turned, F32), (half, F32), (half, F32), (half, F32)],
        [VMEM, VMEM],
        [flat],
        "turn",
    )(z, gates)
    other = swapped(v, 1)
    half4, half5, half6 = swapped(half4, 2), swapped(half5, 6), swapped(half6, 8)
    (hops,) = call(local_hops_kernel, [(turned, F32)], [VMEM, SMEM, SMEM], (), "hops")(v, hop_coef, hop_mask)
    (send,) = call(
        return_kernel,
        [((devices * PACK, LANES), F32)],
        [VMEM] * 5 + [SMEM] * 2 + [VMEM] * 3,
        [pltpu.VMEM(turned, F32), flat],
        "back",
    )(hops, other, half4, half5, half6, hop_coef, hop_mask, u4, z, gates)
    received = exchange(send)
    adjoint, pack = call(
        backward_kernel,
        [((middle, LANES), F32), ((devices * 5, LANES), F32)],
        [VMEM] * 7,
        [flat],
        "backward",
    )(received, x, s1, s2, gates, k_high, k_low)
    factor = 2.0 / (devices * middle)
    upper, pack = call(
        functools.partial(reduce_kernel, factor=factor),
        [((2, LANES, LANES), F32), ((devices * 3, LANES), F32)],
        [VMEM],
        (),
        "reduce",
    )(exchange(pack))
    (grads,) = call(gather_kernel, [((blocks, LANES, LANES), F32)], [VMEM, VMEM], (), "gather")(exchange(pack), upper)
    return adjoint.reshape(initial_state.shape), grads


def solution(mesh):
    return jax.shard_map(
        on_device,
        mesh=mesh,
        in_specs=(P(("runs", AMP), None, None), P("runs", None), P(), P(), P()),
        out_specs=(P(("runs", AMP), None, None), P("runs", None, None)),
        check_vma=False,
    )
```

time: 532 us -> 212 us (0.40); the launches traced: 523 us -> 212 us
  waiting for transfers between devices: 272 us -> 3.81 us
  blocking collectives: 0 us -> 169 us
  local copies, waits for them, and re-layouts: 96.7 us -> 2.37 us
  starting transfers between devices: 56.5 us -> 4.38 us
  other arithmetic: 41.8 us -> 0 us
  matrix products: 40.7 us -> 0 us
  Pallas kernels: 0 us -> 32.1 us
  between operations: 14.9 us -> 0.66 us
    psum x3 -> x0, waiting for transfers between devices: 223 us -> none  [by_axis(): x = lax.psum(x, axis)]
    all_to_all x0 -> x4, blocking collectives: none -> 169 us  [exchange(): lax.all_to_all(shaped, AMP, split_axis=0, concat_axis=0, tiled=True)]
    mul x3 -> x0, local copies, waits for them, and re-layouts: 57.7 us -> none  [apply_local(): widened = jnp.kron(unitary, jnp.eye(4, dtype=unitary.dtype))]
    all_to_all x2 -> x0, waiting for transfers between devices: 48.7 us -> none  [the longest x1 29.1 us: on_device(): lax.all_to_all(current, AMP, split_axis=1, concat_axis=0, tiled=True)]
    dot_general x27 -> x0, matrix products: 40.7 us -> none  [the longest x12 10.2 us: apply_local(): jnp.einsum(apply_forms[window], unitary, shaped, precision=exact_mode)]
    all_to_all x2 -> x0, starting transfers between devices: 40.2 us -> none  [the longest x1 31 us: on_device(): lax.all_to_all(current, AMP, split_axis=1, concat_axis=0, tiled=True)]
    pallas_call x0 -> x7, Pallas kernels: none -> 32.1 us  [the longest x1 12.1 us: on_device(): call(forward_kernel, [((middle, LANES), F32), (wide, F32), (wide, F32), (...]
    mul x5 -> x0, other arithmetic: 26.8 us -> none  [the longest x1 22 us: apply_local(): widened = jnp.kron(unitary, jnp.eye(4, dtype=unitary.dtype))]
  transfers between devices with their start and end apart: 10 -> 4, of which waited for: 5 -> 3; matrix products, arithmetic and copies ran while one was open for 13% -> 0% of each run, Pallas kernels for 0% -> 1%
where the time goes in v1:
time: 212 us
  blocking collectives  169 us (80%)
  Pallas kernels  32.1 us (15%)
  starting transfers between devices  4.38 us (2%)
  waiting for transfers between devices  3.81 us (2%)
  local copies, waits for them, and re-layouts  2.37 us (1%)
    all_to_all x4, blocking collectives, exchange(): lax.all_to_all(shaped, AMP, split_axis=0, concat_axis=0, tiled=True)  169 us
    pallas_call x1, Pallas kernels, on_device(): call(forward_kernel, [((middle, LANES), F32), (wide, F32), (wide, F32), (...  12.1 us
    pallas_call x1, Pallas kernels, on_device(): call(backward_kernel, [((middle, LANES), F32), ((devices * 5, LANES), F32...  5.62 us
    pallas_call x1, Pallas kernels, on_device(): call(return_kernel, [((devices * PACK, LANES), F32)], [VMEM] * 5 + [SMEM]...  4.82 us
    ppermute x4, starting transfers between devices, swapped(): lax.ppermute(value, AMP, [(i, i ^ flip) for i in range(lax.axis_size(AMP))])  4.38 us
  transfers between devices with their start and end apart: 4, of which 3 were waited for; matrix products, arithmetic and copies ran while one was open for 0% of the time, Pallas kernels for 1%

profile of v1, /device:TPU:33, one launch (start us, length us, event | category | flops | bytes accessed | tf_op | source)
XLA Modules:
  0.0 211.9 jit_solution(11340249064026800309)
XLA Ops:
  0.6 0.8 copy.8
  1.4 0.7 reshape.37.pairs
  2.1 12.1 %forward.1 = (f32[1024,128]{1,0:T(8,128)}, f32[256,512]{1,0:T(8,128)}, f32[256,512]{1,0:T(8,128)}, f32[5,128,128]{2,1,0:T(8,128)}, bf16[512,512]{1,0:T(8,128)(2,1)}, /*index=5*/bf16[512,512]{1,0:T(8,128)(2,1)}) custom-call(f32[5,16]{1,0:T(8,128)} %angles.1, s32[160]{0:T(256)} %reshape.37.pairs, f32[1024,128]{1,0:T(8,128)} %bitcast.16), custom_call_target="tpu_custom_call" | custom-call | tf_op jit(solution)/shard_map/forward/pallas_call | solution.py:288
  14.2 61.9 %all_to_all.20 = f32[128,8,1,128]{3,1,2,0:T(8,128)} all-to-all(f32[128,8,1,128]{3,1,2,0:T(8,128)} %bitcast.20), channel_id=1, replica_groups=mesh['runs'=2,'amp'=128] {'amp'}, dimensions={0} | all-to-all | bytes 1048576 | tf_op jit(solution)/shard_map/all_to_all | solution.py:270
  76.1 3.0 %turn.1 = (f32[128,1024]{1,0:T(8,128)}, f32[128,1024]{1,0:T(8,128)}, f32[64,1024]{1,0:T(8,128)}, f32[64,1024]{1,0:T(8,128)}, f32[64,1024]{1,0:T(8,128)}) custom-call(f32[1024,128]{1,0:T(8,128)} %bitcast.12, f32[5,128,128]{2,1,0:T(8,128)} %get-tuple-element.18.gates), custom_call_target="tpu_custom_call" | custom-call | tf_op jit(solution)/shard_map/turn/pallas_call | solution.py:297
  79.0 0.5 collective-permute-start
  79.5 1.4 collective-permute-start.1
  80.9 2.2 %collective-permute-start.2 = (f32[64,1024]{1,0:T(8,128)}, f32[64,1024]{1,0:T(8,128)S(1)}, u32[]{:S(2)}, u32[]{:S(2)}) collective-permute-start(f32[64,1024]{1,0:T(8,128)} %get-tuple-element.21), channel_id=1, source_target_pairs={{0,6},{1,7},{2,4},{3,5},{4,2},{5,3},{6,0},{7,1},{8,14},{9,15},{10,... | collective-permute-start | bytes 786440 | tf_op jit(solution)/shard_map/ppermute | solution.py:274
  83.1 0.3 collective-permute-start.3
  83.4 3.2 %hops.1 = f32[128,1024]{1,0:T(8,128)} custom-call(f32[128,1024]{1,0:T(8,128)} %get-tuple-element.19.v, f32[23]{0:T(128)} %coef.3, s32[23]{0:T(128)} %mask.3), custom_call_target="tpu_custom_call" | custom-call | tf_op jit(solution)/shard_map/hops/pallas_call | solution.py:306
  86.6 0.9 collective-permute-done.1.half4
  87.5 0.0 copy-start.1
  87.5 1.9 collective-permute-done.2.half5
  89.4 0.0 copy-start.2
  89.4 1.0 collective-permute-done.3.half6
  90.4 0.0 copy-start.3
  90.4 0.0 collective-permute-done.other
  90.4 0.0 copy-start
  90.4 0.0 copy-done.1
  90.4 0.0 copy-done.2
  90.4 0.7 copy-done.3
  91.1 0.2 copy-done
  91.3 4.8 %back.1 = f32[1280,128]{1,0:T(8,128)} custom-call(f32[128,1024]{1,0:T(8,128)} %hops.1, f32[128,1024]{1,0:T(8,128)} %copy-done, f32[64,1024]{1,0:T(8,128)} %copy-done.1, f32[64,1024]{1,0:T(8,128)} %copy-done.2, f32[64,1024]{1,0:T(8,128)} %copy-done.3, f32[23]{0:T(128)} %coef.3, s32[23]{0:T(128)} %mask.3, f32[128,1024]{1,0:T(8,128)} %get-tuple-element.23.u4, ...), custom_call_target="tpu_custom_call" | custom-call | tf_op jit(solution)/shard_map/back/pallas_call | solution.py:307
  96.1 45.3 %all_to_all.21 = f32[128,10,1,128]{3,2,1,0:T(1,128)} all-to-all(f32[128,10,1,128]{3,2,1,0:T(1,128)} %bitcast.15), channel_id=1, replica_groups=mesh['runs'=2,'amp'=128] {'amp'}, dimensions={0} | all-to-all | bytes 1310720 | tf_op jit(solution)/shard_map/all_to_all | solution.py:270
  141.4 5.6 %backward.1 = (f32[1024,128]{1,0:T(8,128)}, f32[640,128]{1,0:T(8,128)}) custom-call(f32[1280,128]{1,0:T(8,128)} %bitcast.14, f32[1024,128]{1,0:T(8,128)} %bitcast.17, f32[256,512]{1,0:T(8,128)} %get-tuple-element.24.s1, f32[256,512]{1,0:T(8,128)} %get-tuple-element.25.s2, f32[5,128,128]{2,1,0:T(8,128)} %get-tuple-element.18.gates, ...), custom_call_target="tpu_custom_call" | custom-call | tf_op jit(solution)/shard_map/backward/pallas_call | solution.py:315
  147.0 33.7 %all_to_all.22 = f32[128,5,1,128]{3,2,1,0:T(1,128)} all-to-all(f32[128,5,1,128]{3,2,1,0:T(1,128)} %bitcast.21), channel_id=1, replica_groups=mesh['runs'=2,'amp'=128] {'amp'}, dimensions={0} | all-to-all | bytes 655360 | tf_op jit(solution)/shard_map/all_to_all | solution.py:270
  180.7 1.7 reduce.1
  182.5 27.7 %all_to_all.23 = f32[128,3,1,128]{3,2,1,0:T(1,128)} all-to-all(f32[128,3,1,128]{3,2,1,0:T(1,128)} %bitcast.22), channel_id=1, replica_groups=mesh['runs'=2,'amp'=128] {'amp'}, dimensions={0} | all-to-all | bytes 393216 | tf_op jit(solution)/shard_map/all_to_all | solution.py:270
  210.2 1.7 gather.1
Async XLA Ops:
  79.0 11.4 %collective-permute-start = (f32[128,1024]{1,0:T(8,128)}, f32[128,1024]{1,0:T(8,128)S(1)}, u32[]{:S(2)}, u32[]{:S(2)}) collective-permute-start(f32[128,1024]{1,0:T(8,128)} %get-tuple-element.19.v), channel_id=1, source_target_pairs={{0,1},{1,0},{2,3},{3,2},{4,5},{5,4},{6,7},{7,6},{8,9},{9,8},{10,11... | collective-permute-start | bytes 1572872 | tf_op jit(solution)/shard_map/ppermute | solution.py:274
  79.5 7.9 %collective-permute-start.1 = (f32[64,1024]{1,0:T(8,128)}, f32[64,1024]{1,0:T(8,128)S(1)}, u32[]{:S(2)}, u32[]{:S(2)}) collective-permute-start(f32[64,1024]{1,0:T(8,128)} %get-tuple-element.20), channel_id=1, source_target_pairs={{0,2},{1,3},{2,0},{3,1},{4,6},{5,7},{6,4},{7,5},{8,10},{9,11},{10,... | collective-permute-start | bytes 786440 | tf_op jit(solution)/shard_map/ppermute | solution.py:274
  80.9 8.5 %collective-permute-start.2 = (f32[64,1024]{1,0:T(8,128)}, f32[64,1024]{1,0:T(8,128)S(1)}, u32[]{:S(2)}, u32[]{:S(2)}) collective-permute-start(f32[64,1024]{1,0:T(8,128)} %get-tuple-element.21), channel_id=1, source_target_pairs={{0,6},{1,7},{2,4},{3,5},{4,2},{5,3},{6,0},{7,1},{8,14},{9,15},{10,... | collective-permute-start | bytes 786440 | tf_op jit(solution)/shard_map/ppermute | solution.py:274
  83.1 7.3 %collective-permute-start.3 = (f32[64,1024]{1,0:T(8,128)}, f32[64,1024]{1,0:T(8,128)S(1)}, u32[]{:S(2)}, u32[]{:S(2)}) collective-permute-start(f32[64,1024]{1,0:T(8,128)} %get-tuple-element.22), channel_id=1, source_target_pairs={{0,8},{1,9},{2,10},{3,11},{4,12},{5,13},{6,14},{7,15},{8,0},{9,1},... | collective-permute-start | bytes 786440 | tf_op jit(solution)/shard_map/ppermute | solution.py:274
  87.5 2.9 %copy-start.1 = (f32[64,1024]{1,0:T(8,128)}, f32[64,1024]{1,0:T(8,128)S(1)}, u32[]{:S(2)}) copy-start(f32[64,1024]{1,0:T(8,128)S(1)} %collective-permute-done.1.half4) | copy-start | bytes 786436
  89.4 1.0 copy-start.2
  90.4 0.7 copy-start.3
  90.4 0.9 copy-start

commit v2 on v1

v2 whole, which is shorter than its diff:
```python
import functools

import jax
import jax.numpy as jnp
from jax import lax
from jax.experimental import pallas as pl
from jax.experimental.pallas import tpu as pltpu
from jax.sharding import Mesh
from jax.sharding import PartitionSpec as P

F32, BF16 = jnp.float32, jnp.bfloat16
AMP = ("far", "near")
VMEM = pl.BlockSpec(memory_space=pltpu.VMEM)
SMEM = pl.BlockSpec(memory_space=pltpu.SMEM)

LANES = 128
LOW = 8
PARTS = 4
NEAR = 8
CHAIN_FIRST = 10
RUNG_FIRST = 16


def chunk_of(device):
    return device ^ (((device >> 2) & 1) << 1)


def halves(value):
    high = value.astype(BF16)
    return high, (value - high.astype(F32)).astype(BF16)


def product(left, right, left_dim, right_dim):
    dims = (((left_dim,), (right_dim,)), ((), ()))
    dot = lambda a, b: lax.dot_general(a, b, dims, preferred_element_type=F32)
    return dot(left[0], right[0]) + (dot(left[0], right[1]) + dot(left[1], right[0]))


def own_bits():
    chunk = chunk_of(lax.axis_index(AMP))
    return [(chunk >> k) & 1 for k in range(4)]


def spread_selector():
    rows = lax.broadcasted_iota(jnp.int32, (PARTS * LANES, LANES), 0)
    columns = lax.broadcasted_iota(jnp.int32, (PARTS * LANES, LANES), 1)
    return ((rows >> 2) == columns).astype(F32).astype(BF16)


def same_part():
    shape = (PARTS * LANES, PARTS * LANES)
    rows = lax.broadcasted_iota(jnp.int32, shape, 0)
    columns = lax.broadcasted_iota(jnp.int32, shape, 1)
    return ((rows ^ columns) & (PARTS - 1)) == 0


def forward_kernel(angles, pairs, x_far, send, x, s1_high, s1_low, s2_high, s2_low, gates, k_high, k_low, level_high, level_low, nat, arrived):
    load = pltpu.make_async_copy(x_far, x, arrived)
    load.start()
    block_count, rotation_count = angles.shape
    cosines = jnp.cos(angles[...])
    sines = jnp.sin(angles[...])
    lane = lax.broadcasted_iota(jnp.int32, (LOW, LANES), 1)
    apart = lax.broadcasted_iota(jnp.int32, (LANES, LANES), 0) ^ lax.broadcasted_iota(jnp.int32, (LANES, LANES), 1)

    def turn_of(b, g):
        first, second = pairs[b, 0, g], pairs[b, 1, g]
        cosine = jnp.broadcast_to(cosines[b : b + 1, g : g + 1], lane.shape)
        sine = jnp.broadcast_to(sines[b : b + 1, g : g + 1], lane.shape)

        def at(index):
            one = (index >> first) & 1
            differ = one != ((index >> second) & 1)
            off = jnp.where(differ, jnp.where(one == 1, sine, -sine), 0.0)
            return jnp.where(differ, cosine, 1.0), off

        return (1 << first) | (1 << second), at

    def tall(value):
        return jnp.broadcast_to(value[0:1, :], (LANES, LANES))

    for b in range(block_count):
        for i in range(rotation_count // 2):
            flip1, at1 = turn_of(b, 2 * i)
            flip2, at2 = turn_of(b, 2 * i + 1)
            keep1, cross1 = at1(lane)
            keep2, cross2 = at2(lane)
            keep12, cross12 = at1(lane ^ flip2)
            total = jnp.where(apart == 0, tall(keep2 * keep1), 0.0)
            total = total + jnp.where(apart == flip1, tall(keep2 * cross1), 0.0)
            total = total + jnp.where(apart == flip2, tall(cross2 * keep12), 0.0)
            total = total + jnp.where(apart == (flip1 ^ flip2), tall(cross2 * cross12), 0.0)
            level_high[b, i], level_low[b, i] = halves(total)
    width = rotation_count // 2
    while width > 1:
        width //= 2
        for b in range(block_count):
            for i in range(width):
                left = (level_high[b, 2 * i], level_low[b, 2 * i])
                right = (level_high[b, 2 * i + 1], level_low[b, 2 * i + 1])
                high, low = halves(product(left, right, 1, 0))
                if width > 1:
                    level_high[b, i], level_low[b, i] = high, low
                else:
                    gates[b], gates[block_count + b] = high, low

    pick = spread_selector()
    keep = same_part()
    for out, source in ((k_high, gates[1]), (k_low, gates[block_count + 1])):
        spread = jnp.dot(pick, source, preferred_element_type=F32).astype(BF16)
        wide = lax.dot_general(spread, pick, (((1,), (1,)), ((), ())), preferred_element_type=F32)
        out[...] = jnp.where(keep, wide, 0.0).astype(BF16)
    load.wait()
    g0 = gate(gates, 0)
    for q in range(PARTS):
        part = x[pl.ds(q, x.shape[0] // PARTS, stride=PARTS), :]
        columns = slice(q * LANES, (q + 1) * LANES)
        s1_high[:, columns], s1_low[:, columns] = halves(product(halves(part), g0, 1, 0))
    s2_high[...], s2_low[...] = halves(product((s1_high[...], s1_low[...]), (k_high[...], k_low[...]), 1, 0))
    g2 = gate(gates, 2)
    for e in range(s2_high.shape[0] // LANES):
        rows = slice(e * LANES, (e + 1) * LANES)
        s3 = product(g2, (s2_high[rows, :], s2_low[rows, :]), 0, 0)
        for q in range(PARTS):
            nat[pl.ds(e * PARTS * LANES + q, LANES, stride=PARTS), :] = s3[:, q * LANES : (q + 1) * LANES]
    for d in range(send.shape[0] // LOW):
        c = chunk_of(d)
        send[d * LOW : (d + 1) * LOW, :] = nat[c * LOW : (c + 1) * LOW, :]


def gate(gates, number):
    return gates[number], gates[gates.shape[0] // 2 + number]


def turn_kernel(z, gates, v, u4_high, u4_low, half4, half5, half6, scratch):
    bits = own_bits()
    g3 = gate(gates, 3)
    for block in range(z.shape[0] // LANES):
        rows = slice(block * LANES, (block + 1) * LANES)
        scratch[rows, :] = product(g3, halves(z[rows, :]), 0, 0)
    for c in range(LOW):
        columns = slice(c * LANES, (c + 1) * LANES)
        u4_high[:, columns], u4_low[:, columns] = halves(scratch[pl.ds(c, LANES, stride=LOW), :])
    v[...] = product(gate(gates, 4), (u4_high[...], u4_low[...]), 0, 0)
    for out, k in ((half4, 4), (half5, 5), (half6, 6)):
        size = 1 << k
        for j in range(LANES // (2 * size)):
            start = pl.multiple_of(j * 2 * size + (1 - bits[k - 3]) * size, size)
            out[j * size : (j + 1) * size, :] = v[pl.ds(start, size), :]


def weight(coef, mask, number):
    return coef[number] * mask[number].astype(F32)


def pair_matrix(low, high, scale):
    rows = lax.broadcasted_iota(jnp.int32, (LANES, LANES), 0)
    columns = lax.broadcasted_iota(jnp.int32, (LANES, LANES), 1)
    active = (((rows >> low) ^ (rows >> high)) & 1) == 1
    return jnp.where(active & ((rows ^ columns) == ((1 << low) | (1 << high))), scale, 0.0)


def local_hops_kernel(v, coef, mask, out):
    lane_chain = sum(pair_matrix(k, k + 1, weight(coef, mask, k)) for k in range(6))
    top_chain = sum(pair_matrix(k, k + 1, weight(coef, mask, CHAIN_FIRST + k)) for k in range(6))
    lane_chain, top_chain = halves(lane_chain), halves(top_chain)
    rows = lax.broadcasted_iota(jnp.int32, (LANES, LANES), 0)
    columns = lax.broadcasted_iota(jnp.int32, (LANES, LANES), 1)
    rungs = []
    for k in range(3):
        scale = weight(coef, mask, RUNG_FIRST + k)
        paired = (rows ^ columns) == (1 << k)
        rungs.append([halves(jnp.where(paired & (((rows >> k) & 1) == 1 - c), scale, 0.0)) for c in range(2)])
    blocks = [v[:, c * LANES : (c + 1) * LANES] for c in range(LOW)]
    parts = [halves(block) for block in blocks]
    for c in range(LOW):
        total = product(parts[c], lane_chain, 1, 0) + product(top_chain, parts[c], 1, 0)
        for k in range(3):
            total = total + product(rungs[k][(c >> k) & 1], parts[c ^ (1 << k)], 1, 0)
        moved = pltpu.roll(blocks[c ^ 1], LANES // 2, 1)
        wanted = (columns >> 6) == 1 - (c & 1)
        total = total + jnp.where(wanted, weight(coef, mask, 6) * moved, 0.0)
        for k in range(2):
            if (c >> k) & 1 != (c >> (k + 1)) & 1:
                total = total + weight(coef, mask, 7 + k) * blocks[c ^ (3 << k)]
        out[:, c * LANES : (c + 1) * LANES] = total


def return_kernel(hops, other, half4, half5, half6, coef, mask, u4_high, u4_low, z, gates, send, grams, lam, scratch):
    bits = own_bits()
    lam[...] = hops[...]
    wide = lam.shape[1] // 2
    to = pl.multiple_of((1 - bits[0]) * wide, wide)
    source = pl.multiple_of(bits[0] * wide, wide)
    lam[:, pl.ds(to, wide)] += weight(coef, mask, 9) * other[:, pl.ds(source, wide)]
    for j in range(LANES // 16):
        to = pl.multiple_of(j * 16 + (1 - bits[0]) * 8, 8)
        source = pl.multiple_of(j * 16 + bits[0] * 8, 8)
        lam[pl.ds(to, 8), :] += weight(coef, mask, RUNG_FIRST + 3) * other[pl.ds(source, 8), :]
    for half, k in ((half4, 4), (half5, 5), (half6, 6)):
        size = 1 << k
        for j in range(LANES // (2 * size)):
            to = pl.multiple_of(j * 2 * size + (1 - bits[k - 3]) * size, size)
            lam[pl.ds(to, size), :] += weight(coef, mask, RUNG_FIRST + k) * half[j * size : (j + 1) * size, :]
    lam5 = halves(lam[...])
    grams[1] = product(lam5, (u4_high[...], u4_low[...]), 1, 1)
    lam4 = product(gate(gates, 4), lam5, 1, 0)
    for c in range(LOW):
        scratch[pl.ds(c, LANES, stride=LOW), :] = lam4[:, c * LANES : (c + 1) * LANES]
    g3 = gate(gates, 3)
    gram = jnp.zeros((LANES, LANES), F32)
    for block in range(z.shape[0] // LANES):
        rows = slice(block * LANES, (block + 1) * LANES)
        inner = halves(scratch[rows, :])
        gram = gram + product(inner, halves(z[rows, :]), 1, 1)
        send[rows, :] = product(g3, inner, 1, 0)
    grams[0] = gram


def backward_kernel(received, x, s1_high, s1_low, s2_high, s2_low, gates, k_high, k_low, upper, adjoint, pack, nat):
    for d in range(received.shape[0] // LOW):
        c = chunk_of(d)
        nat[c * LOW : (c + 1) * LOW, :] = received[d * LOW : (d + 1) * LOW, :]
    count = x.shape[0] // PARTS
    g2 = gate(gates, 2)
    gram2 = jnp.zeros((LANES, LANES), F32)
    pieces = []
    for e in range(count // LANES):
        rows = slice(e * LANES, (e + 1) * LANES)
        lam3 = jnp.concatenate(
            [nat[pl.ds(e * PARTS * LANES + q, LANES, stride=PARTS), :] for q in range(PARTS)], axis=1
        )
        lam3 = halves(lam3)
        gram2 = gram2 + product(lam3, (s2_high[rows, :], s2_low[rows, :]), 1, 1)
        pieces.append(product(g2, lam3, 1, 0))
    lam2 = halves(jnp.concatenate(pieces, axis=0))
    wide = jnp.where(same_part(), product(lam2, (s1_high[...], s1_low[...]), 0, 0), 0.0)
    pick = spread_selector()
    dims = (((0,), (0,)), ((), ()))
    high, low = halves(wide)
    dot = functools.partial(lax.dot_general, preferred_element_type=F32)
    folded = dot(pick, high, dims) + dot(pick, low, dims)
    high, low = halves(folded)
    gram1 = jnp.dot(high, pick, preferred_element_type=F32) + jnp.dot(low, pick, preferred_element_type=F32)
    lam1 = product(lam2, (k_high[...], k_low[...]), 1, 1)
    g0 = gate(gates, 0)
    gram0 = jnp.zeros((LANES, LANES), F32)
    for q in range(PARTS):
        inner = halves(lam1[:, q * LANES : (q + 1) * LANES])
        gram0 = gram0 + product(inner, halves(x[pl.ds(q, count, stride=PARTS), :]), 0, 0)
        adjoint[pl.ds(q, count, stride=PARTS), :] = product(inner, g0, 1, 1)
    size = LANES // NEAR
    total = 5 * size
    for k, gram in enumerate((gram0, gram1, gram2, upper[0], upper[1])):
        for d in range(NEAR):
            pack[d * total + k * size : d * total + (k + 1) * size, :] = gram[d * size : (d + 1) * size, :]


def near_sum_kernel(received, pack):
    total = received.shape[0] // NEAR
    size = total // 5
    value = received[0:total, :]
    for d in range(1, NEAR):
        value = value + received[d * total : (d + 1) * total, :]
    for k in range(5):
        pack[pl.ds(k, size, stride=5), :] = value[k * size : (k + 1) * size, :]


def far_sum_kernel(received, pack, *, factor):
    size = received.shape[0] // 5
    for k in range(5):
        mine = jnp.sum(received[pl.ds(k, size, stride=5), :], axis=0, keepdims=True)
        pack[pl.ds(k, size, stride=5), :] = jnp.broadcast_to(factor * mine, (size, LANES))


def hand_out_kernel(received, pack):
    total = received.shape[0]
    size = total // 5
    for k in range(5):
        rows = received[pl.ds(k, size, stride=5), :]
        for d in range(NEAR):
            pack[d * total + k * size : d * total + (k + 1) * size, :] = rows


def gather_kernel(received, grads):
    total = received.shape[0] // NEAR
    size = total // 5
    for k in range(5):
        for d in range(NEAR):
            grads[k, d * size : (d + 1) * size, :] = received[d * total + k * size : d * total + (k + 1) * size, :]


def call(kernel, outs, specs, scratch=(), name=None):
    made = pl.pallas_call(
        kernel,
        out_shape=[
            jax.ShapeDtypeStruct(out[0], out[1]) if len(out) > 2 else pltpu.VMEM(out[0], out[1]) for out in outs
        ],
        in_specs=specs,
        out_specs=[VMEM] * len(outs),
        scratch_shapes=list(scratch),
        compiler_params=pltpu.CompilerParams(vmem_limit_bytes=24 << 20),
        name=name,
    )

    def run(*operands):
        kept = [
            pltpu.with_memory_space_constraint(operand, pltpu.VMEM) if spec is VMEM else operand
            for operand, spec in zip(operands, specs)
        ]
        return made(*kept)

    return run


def exchange(rows, axes):
    devices = lax.axis_size(axes)
    shaped = rows.reshape(devices, rows.shape[0] // devices, 1, rows.shape[1])
    return lax.all_to_all(shaped, axes, split_axis=0, concat_axis=0, tiled=True).reshape(rows.shape)


def swapped(value, flip):
    return lax.ppermute(value, AMP, [(i, i ^ flip) for i in range(lax.axis_size(AMP))])


def on_device(initial_state, gate_angles, gate_pairs, hop_coef, hop_mask):
    devices = lax.axis_size(AMP)
    middle = initial_state.shape[1]
    x = initial_state.reshape(middle, LANES)
    blocks, rotations = gate_angles.shape
    wide = (middle // PARTS, PARTS * LANES)
    turned = (devices, LOW * LANES)
    half = (devices // 2, LOW * LANES)
    square = (PARTS * LANES, PARTS * LANES)
    level = pltpu.VMEM((blocks, rotations // 2, LANES, LANES), BF16)
    flat = pltpu.VMEM((middle, LANES), F32)

    send, x_near, s1_high, s1_low, s2_high, s2_low, gates, k_high, k_low = call(
        forward_kernel,
        [((middle, LANES), F32)] * 2
        + [(wide, BF16)] * 4
        + [((2 * blocks, LANES, LANES), BF16)]
        + [(square, BF16)] * 2,
        [VMEM, SMEM, pl.BlockSpec(memory_space=pl.ANY)],
        [level, level, flat, pltpu.SemaphoreType.DMA],
        "forward",
    )(gate_angles, jnp.swapaxes(gate_pairs, 1, 2), x)
    z = exchange(send, AMP)
    v, u4_high, u4_low, half4, half5, half6 = call(
        turn_kernel,
        [(turned, F32), (turned, BF16), (turned, BF16), (half, F32), (half, F32), (half, F32)],
        [VMEM, VMEM],
        [flat],
        "turn",
    )(z, gates)
    other = swapped(v, 1)
    half4, half5, half6 = swapped(half4, 2), swapped(half5, 6), swapped(half6, 8)
    (hops,) = call(local_hops_kernel, [(turned, F32)], [VMEM, SMEM, SMEM], (), "hops")(v, hop_coef, hop_mask)
    send, upper = call(
        return_kernel,
        [((middle, LANES), F32), ((2, LANES, LANES), F32)],
        [VMEM] * 5 + [SMEM] * 2 + [VMEM] * 4,
        [pltpu.VMEM(turned, F32), flat],
        "back",
    )(hops, other, half4, half5, half6, hop_coef, hop_mask, u4_high, u4_low, z, gates)
    received = exchange(send, AMP)
    pack = ((5 * LANES, LANES), F32)
    rows = ((5 * LANES // NEAR, LANES), F32)
    adjoint, partial = call(backward_kernel, [((middle, LANES), F32), pack], [VMEM] * 10, [flat], "backward")(
        received, x_near, s1_high, s1_low, s2_high, s2_low, gates, k_high, k_low, upper
    )
    (partial,) = call(near_sum_kernel, [rows], [VMEM], (), "near")(exchange(partial, "near"))
    far_sum = functools.partial(far_sum_kernel, factor=2.0 / (devices * middle))
    (sums,) = call(far_sum, [rows], [VMEM], (), "far")(exchange(partial, "far"))
    (sums,) = call(hand_out_kernel, [pack], [VMEM], (), "hand")(exchange(sums, "far"))
    (grads,) = call(gather_kernel, [((blocks, LANES, LANES), F32, True)], [VMEM], (), "gather")(exchange(sums, "near"))
    return adjoint.reshape(initial_state.shape), grads


def solution(mesh):
    runs, amp = mesh.shape["runs"], mesh.shape["amp"]
    split = Mesh(mesh.devices.reshape(runs, amp // NEAR, NEAR), ("runs",) + AMP)
    return jax.shard_map(
        on_device,
        mesh=split,
        in_specs=(P(("runs",) + AMP, None, None), P("runs", None), P(), P(), P()),
        out_specs=(P(("runs",) + AMP, None, None), P("runs", None, None)),
        check_vma=False,
    )
```

time: 212 us -> 185 us (0.87)
  blocking collectives: 169 us -> 143 us
  Pallas kernels: 32.1 us -> 14.7 us
  waiting for transfers between devices: 3.81 us -> 11.2 us
  starting transfers between devices: 4.38 us -> 11.4 us
    all_to_all x4 -> x5, blocking collectives: 169 us -> 143 us  [exchange(): lax.all_to_all(shaped, axes, split_axis=0, concat_axis=0, tiled=True)]
    pallas_call x7 -> x9, Pallas kernels: 32.1 us -> 14.7 us  [run(): return made(*kept)]
    all_to_all x0 -> x1, starting transfers between devices: none -> 6.69 us  [exchange(): lax.all_to_all(shaped, axes, split_axis=0, concat_axis=0, tiled=True)]
    all_to_all x0 -> x1, waiting for transfers between devices: none -> 6.37 us  [exchange(): lax.all_to_all(shaped, axes, split_axis=0, concat_axis=0, tiled=True)]
  transfers between devices with their start and end apart: 4 -> 5, of which waited for: 3 -> 4; matrix products, arithmetic and copies ran while one was open for 0% -> 0% of each run, Pallas kernels for 1% -> 1%
where the time goes in v2:
time: 185 us; the launch traced here: 184 us
  blocking collectives  143 us (77%)
  Pallas kernels  14.7 us (8%)
  starting transfers between devices  11.4 us (6%)
  waiting for transfers between devices  11.2 us (6%)
  local copies, waits for them, and re-layouts  3.21 us (2%)
    all_to_all x5, blocking collectives, exchange(): lax.all_to_all(shaped, axes, split_axis=0, concat_axis=0, tiled=True)  143 us
    pallas_call x9, Pallas kernels, run(): return made(*kept)  14.7 us
    all_to_all x1, starting transfers between devices, exchange(): lax.all_to_all(shaped, axes, split_axis=0, concat_axis=0, tiled=True)  6.69 us
    all_to_all x1, waiting for transfers between devices, exchange(): lax.all_to_all(shaped, axes, split_axis=0, concat_axis=0, tiled=True)  6.37 us
    ppermute x4, waiting for transfers between devices, swapped(): lax.ppermute(value, AMP, [(i, i ^ flip) for i in range(lax.axis_size(AMP))])  4.83 us
    ppermute x4, starting transfers between devices, swapped(): lax.ppermute(value, AMP, [(i, i ^ flip) for i in range(lax.axis_size(AMP))])  4.67 us
  transfers between devices with their start and end apart: 5, of which 4 were waited for; matrix products, arithmetic and copies ran while one was open for 0% of the time, Pallas kernels for 1%

profile of v2, /device:TPU:33, one launch (start us, length us, event | category | flops | bytes accessed | tf_op | source)
XLA Modules:
  0.0 184.3 jit_solution(2011142331554698576)
XLA Ops:
  0.6 0.0 copy-start
  0.6 1.0 copy-done
  1.7 0.0 copy-start.1
  1.7 0.7 copy-done.1
  2.4 0.0 copy-start.2
  2.4 0.7 copy-done.2
  3.0 5.1 %forward.1 = (f32[1024,128]{1,0:T(8,128)S(1)}, f32[1024,128]{1,0:T(8,128)S(1)}, bf16[256,512]{1,0:T(8,128)(2,1)S(1)}, bf16[256,512]{1,0:T(8,128)(2,1)S(1)}, bf16...) custom-call(f32[5,16]{1,0:T(8,128)S(1)} %copy-done.2, ...), custom_call_target="tpu_custom_call" | custom-call | tf_op jit(solution)/shard_map/forward/pallas_call | solution.py:311
  8.1 61.5 %all_to_all.30 = f32[128,8,1,128]{3,1,2,0:T(8,128)S(1)} all-to-all(f32[128,8,1,128]{3,1,2,0:T(8,128)S(1)} %bitcast.31), channel_id=1, replica_groups=mesh['runs'=2,'far'=16,'near'=8] {'far','near'}, dimensions={0} | all-to-all | bytes 1048576 | tf_op jit(solution)/shard_map/all_to_all | solution.py:319
  69.7 0.9 turn.1
  70.5 0.6 collective-permute-start
  71.2 1.5 collective-permute-start.1
  72.7 0.0 copy-start.3
  72.7 2.1 %collective-permute-start.2 = (f32[64,1024]{1,0:T(8,128)S(1)}, f32[64,1024]{1,0:T(8,128)S(1)}, u32[]{:S(2)}, u32[]{:S(2)}) collective-permute-start(f32[64,1024]{1,0:T(8,128)S(1)} %get-tuple-element.25), channel_id=1, source_target_pairs={{0,6},{1,7},{2,4},{3,5},{4,2},{5,3},{6,0},{7,1},{8,14},{9,15},{10,... | collective-permute-start | bytes 786440 | tf_op jit(solution)/shard_map/ppermute | solution.py:323
  74.7 0.5 collective-permute-start.3
  75.2 0.0 copy-done.3
  75.2 0.0 copy-done.4
  75.2 1.9 %hops.1 = f32[128,1024]{1,0:T(8,128)S(1)} custom-call(f32[128,1024]{1,0:T(8,128)S(1)} %get-tuple-element.23.v, f32[23]{0:T(128)S(1)} %copy-done.3, s32[23]{0:T(128)S(1)} %copy-done.4), custom_call_target="tpu_custom_call" | custom-call | tf_op jit(solution)/shard_map/hops/pallas_call | solution.py:311
  77.1 1.9 %collective-permute-done.1.half4 = f32[64,1024]{1,0:T(8,128)S(1)} collective-permute-done((f32[64,1024]{1,0:T(8,128)S(1)}, f32[64,1024]{1,0:T(8,128)S(1)}, u32[]{:S(2)}, u32[]{:S(2)}) %collective-permute-start.1) | collective-permute-done | bytes 262176 | tf_op jit(solution)/shard_map/ppermute | solution.py:323
  79.0 2.1 %collective-permute-done.2.half5 = f32[64,1024]{1,0:T(8,128)S(1)} collective-permute-done((f32[64,1024]{1,0:T(8,128)S(1)}, f32[64,1024]{1,0:T(8,128)S(1)}, u32[]{:S(2)}, u32[]{:S(2)}) %collective-permute-start.2) | collective-permute-done | bytes 262176 | tf_op jit(solution)/shard_map/ppermute | solution.py:323
  81.1 0.8 collective-permute-done.3.half6
  81.9 0.0 collective-permute-done.other
  81.9 2.6 %back.1 = (f32[1024,128]{1,0:T(8,128)S(1)}, f32[2,128,128]{2,1,0:T(8,128)S(1)}) custom-call(f32[128,1024]{1,0:T(8,128)S(1)} %hops.1, f32[128,1024]{1,0:T(8,128)S(1)} %collective-permute-done.other, f32[64,1024]{1,0:T(8,128)S(1)} %collective-permute-done.1.half4, f32[64,1024]{1,0:T(8,128)S(1)} %collective-permute-done.2.half5, ...), custom_call_target="tpu_custom_call" | custom-call | tf_op jit(solution)/shard_map/back/pallas_call | solution.py:311
  84.6 40.2 %all_to_all.31 = f32[128,8,1,128]{3,1,2,0:T(8,128)S(1)} all-to-all(f32[128,8,1,128]{3,1,2,0:T(8,128)S(1)} %bitcast.30), channel_id=1, replica_groups=mesh['runs'=2,'far'=16,'near'=8] {'far','near'}, dimensions={0} | all-to-all | bytes 1048576 | tf_op jit(solution)/shard_map/all_to_all | solution.py:319
  124.8 2.8 %backward.1 = (f32[1024,128]{1,0:T(8,128)S(1)}, f32[640,128]{1,0:T(8,128)S(1)}) custom-call(f32[1024,128]{1,0:T(8,128)S(1)} %bitcast.26, f32[1024,128]{1,0:T(8,128)S(1)} %get-tuple-element.30.x, bf16[256,512]{1,0:T(8,128)(2,1)S(1)} %get-tuple-element.31.s1_high, bf16[256,512]{1,0:T(8,128)(2,1)S(1)} %get-tuple-element.32.s1_low, ...), custom_call_target="tpu_custom_call" | custom-call | tf_op jit(solution)/shard_map/backward/pallas_call | solution.py:311
  127.6 12.9 %all_to_all.32 = f32[8,80,1,128]{3,1,2,0:T(8,128)S(1)} all-to-all(f32[8,80,1,128]{3,1,2,0:T(8,128)S(1)} %bitcast.32), channel_id=1, replica_groups=mesh['runs'=2,'far'=16,'near'=8] {'near'}, dimensions={0} | all-to-all | bytes 655360 | tf_op jit(solution)/shard_map/all_to_all | solution.py:319
  140.4 14.3 %all_to_all.33 = f32[16,5,1,128]{3,2,1,0:T(1,128)S(1)} all-to-all(f32[16,5,1,128]{3,2,1,0:T(1,128)S(1)} %bitcast.35), channel_id=1, replica_groups=mesh['runs'=2,'far'=16,'near'=8] {'far'}, dimensions={0} | all-to-all | bytes 81920 | tf_op jit(solution)/shard_map/all_to_all | solution.py:319
  154.8 14.1 %all_to_all.34 = f32[16,5,1,128]{3,2,1,0:T(1,128)S(1)} all-to-all(f32[16,5,1,128]{3,2,1,0:T(1,128)S(1)} %bitcast.34), channel_id=1, replica_groups=mesh['runs'=2,'far'=16,'near'=8] {'far'}, dimensions={0} | all-to-all | bytes 81920 | tf_op jit(solution)/shard_map/all_to_all | solution.py:319
  169.0 0.7 hand.1
  169.7 6.7 %all-to-all-start.5 = ((f32[8,80,1,128]{3,1,2,0:T(8,128)}), f32[8,80,1,128]{3,1,2,0:T(8,128)S(1)}, u32[]{:S(2)}, u32[]{:S(2)}) async-start(f32[8,80,1,128]{3,1,2,0:T(8,128)} %bitcast.17), calls=%async_computation.5 | async-start | bytes 655360 | tf_op jit(solution)/shard_map/all_to_all | solution.py:319
  176.4 0.8 copy.13
  177.2 6.4 %all-to-all-done.5 = f32[8,80,1,128]{3,1,2,0:T(8,128)S(1)} async-done(((f32[8,80,1,128]{3,1,2,0:T(8,128)}), f32[8,80,1,128]{3,1,2,0:T(8,128)S(1)}, u32[]{:S(2)}, u32[]{:S(2)}) %all-to-all-start.5) | async-done | bytes 327712 | tf_op jit(solution)/shard_map/all_to_all | solution.py:319
  183.6 0.7 gather.1
  (3 shorter events, 0.0 us)
Async XLA Ops:
  0.6 1.0 copy-start
  1.7 0.7 copy-start.1
  2.4 0.7 copy-start.2
  70.5 11.4 %collective-permute-start = (f32[128,1024]{1,0:T(8,128)S(1)}, f32[128,1024]{1,0:T(8,128)S(1)}, u32[]{:S(2)}, u32[]{:S(2)}) collective-permute-start(f32[128,1024]{1,0:T(8,128)S(1)} %get-tuple-element.23.v), channel_id=1, source_target_pairs={{0,1},{1,0},{2,3},{3,2},{4,5},{5,4},{6,7},{7,6},{8,9},{9,8},{10,11... | collective-permute-start | bytes 1572872 | tf_op jit(solution)/shard_map/ppermute | solution.py:323
  71.2 7.9 %collective-permute-start.1 = (f32[64,1024]{1,0:T(8,128)S(1)}, f32[64,1024]{1,0:T(8,128)S(1)}, u32[]{:S(2)}, u32[]{:S(2)}) collective-permute-start(f32[64,1024]{1,0:T(8,128)S(1)} %get-tuple-element.24), channel_id=1, source_target_pairs={{0,2},{1,3},{2,0},{3,1},{4,6},{5,7},{6,4},{7,5},{8,10},{9,11},{10,... | collective-permute-start | bytes 786440 | tf_op jit(solution)/shard_map/ppermute | solution.py:323
  72.7 2.5 %copy-start.3 = (f32[23]{0:T(128)S(1)}, f32[23]{0:T(128)}, u32[]{:S(2)}) copy-start(f32[23]{0:T(128)} %coef.3) | copy-start | bytes 280
  72.7 2.5 %copy-start.4 = (s32[23]{0:T(128)S(1)}, s32[23]{0:T(128)}, u32[]{:S(2)}) copy-start(s32[23]{0:T(128)} %mask.3) | copy-start | bytes 280
  72.7 8.4 %collective-permute-start.2 = (f32[64,1024]{1,0:T(8,128)S(1)}, f32[64,1024]{1,0:T(8,128)S(1)}, u32[]{:S(2)}, u32[]{:S(2)}) collective-permute-start(f32[64,1024]{1,0:T(8,128)S(1)} %get-tuple-element.25), channel_id=1, source_target_pairs={{0,6},{1,7},{2,4},{3,5},{4,2},{5,3},{6,0},{7,1},{8,14},{9,15},{10,... | collective-permute-start | bytes 786440 | tf_op jit(solution)/shard_map/ppermute | solution.py:323
  74.7 7.2 %collective-permute-start.3 = (f32[64,1024]{1,0:T(8,128)S(1)}, f32[64,1024]{1,0:T(8,128)S(1)}, u32[]{:S(2)}, u32[]{:S(2)}) collective-permute-start(f32[64,1024]{1,0:T(8,128)S(1)} %get-tuple-element.26), channel_id=1, source_target_pairs={{0,8},{1,9},{2,10},{3,11},{4,12},{5,13},{6,14},{7,15},{8,0},{9,1},... | collective-permute-start | bytes 786440 | tf_op jit(solution)/shard_map/ppermute | solution.py:323
  169.7 13.9 %all-to-all-start.5 = ((f32[8,80,1,128]{3,1,2,0:T(8,128)}), f32[8,80,1,128]{3,1,2,0:T(8,128)S(1)}, u32[]{:S(2)}, u32[]{:S(2)}) async-start(f32[8,80,1,128]{3,1,2,0:T(8,128)} %bitcast.17), calls=%async_computation.5 | async-start | bytes 655360 | tf_op jit(solution)/shard_map/all_to_all | solution.py:319

commit v3 on v2

--- a/solution.py
+++ b/solution.py
@@ -12,11 +12,12 @@
 AMP = ("far", "near")
 VMEM = pl.BlockSpec(memory_space=pltpu.VMEM)
 SMEM = pl.BlockSpec(memory_space=pltpu.SMEM)
+FAR = pl.BlockSpec(memory_space=pltpu.HBM)
 
 LANES = 128
 LOW = 8
 PARTS = 4
-NEAR = 8
+NEAR = 16
 CHAIN_FIRST = 10
 RUNG_FIRST = 16
 
@@ -54,9 +55,19 @@
     return ((rows ^ columns) & (PARTS - 1)) == 0
 
 
-def forward_kernel(angles, pairs, x_far, send, x, s1_high, s1_low, s2_high, s2_low, gates, k_high, k_low, level_high, level_low, nat, arrived):
-    load = pltpu.make_async_copy(x_far, x, arrived)
-    load.start()
+def forward_kernel(
+    angles_far, pairs_far, x_far, send, x, s1_high, s1_low, s2_high, s2_low, gates, k_high, k_low,
+    level_high, level_low, nat, angles, pairs, arrived,
+):
+    small = [
+        pltpu.make_async_copy(angles_far, angles, arrived.at[0]),
+        pltpu.make_async_copy(pairs_far, pairs, arrived.at[1]),
+    ]
+    load = pltpu.make_async_copy(x_far, x, arrived.at[2])
+    for copy in small + [load]:
+        copy.start()
+    for copy in small:
+        copy.wait()
     block_count, rotation_count = angles.shape
     cosines = jnp.cos(angles[...])
     sines = jnp.sin(angles[...])
@@ -256,38 +267,21 @@
             pack[d * total + k * size : d * total + (k + 1) * size, :] = gram[d * size : (d + 1) * size, :]
 
 
-def near_sum_kernel(received, pack):
-    total = received.shape[0] // NEAR
-    size = total // 5
-    value = received[0:total, :]
-    for d in range(1, NEAR):
-        value = value + received[d * total : (d + 1) * total, :]
-    for k in range(5):
-        pack[pl.ds(k, size, stride=5), :] = value[k * size : (k + 1) * size, :]
-
-
-def far_sum_kernel(received, pack, *, factor):
-    size = received.shape[0] // 5
-    for k in range(5):
-        mine = jnp.sum(received[pl.ds(k, size, stride=5), :], axis=0, keepdims=True)
-        pack[pl.ds(k, size, stride=5), :] = jnp.broadcast_to(factor * mine, (size, LANES))
-
-
-def hand_out_kernel(received, pack):
-    total = received.shape[0]
-    size = total // 5
-    for k in range(5):
-        rows = received[pl.ds(k, size, stride=5), :]
-        for d in range(NEAR):
-            pack[d * total + k * size : d * total + (k + 1) * size, :] = rows
+def sum_and_copy_kernel(received, pack, *, sources, factor):
+    size = received.shape[0] // sources
+    value = received[0:size, :]
+    for d in range(1, sources):
+        value = value + received[d * size : (d + 1) * size, :]
+    for d in range(pack.shape[0] // size):
+        pack[d * size : (d + 1) * size, :] = factor * value
 
 
 def gather_kernel(received, grads):
-    total = received.shape[0] // NEAR
-    size = total // 5
-    for k in range(5):
-        for d in range(NEAR):
-            grads[k, d * size : (d + 1) * size, :] = received[d * total + k * size : d * total + (k + 1) * size, :]
+    size = LANES // NEAR
+    for d in range(NEAR):
+        for k in range(5):
+            start = (d * 5 + k) * size
+            grads[k, d * size : (d + 1) * size, :] = received[start : start + size, :]
 
 
 def call(kernel, outs, specs, scratch=(), name=None):
@@ -305,7 +299,9 @@
 
     def run(*operands):
         kept = [
-            pltpu.with_memory_space_constraint(operand, pltpu.VMEM) if spec is VMEM else operand
+            operand
+            if spec is SMEM
+            else pltpu.with_memory_space_constraint(operand, pltpu.HBM if spec is FAR else pltpu.VMEM)
             for operand, spec in zip(operands, specs)
         ]
         return made(*kept)
@@ -341,8 +337,15 @@
         + [(wide, BF16)] * 4
         + [((2 * blocks, LANES, LANES), BF16)]
         + [(square, BF16)] * 2,
-        [VMEM, SMEM, pl.BlockSpec(memory_space=pl.ANY)],
-        [level, level, flat, pltpu.SemaphoreType.DMA],
+        [FAR] * 3,
+        [
+            level,
+            level,
+            flat,
+            pltpu.VMEM(gate_angles.shape, F32),
+            pltpu.SMEM((blocks, 2, rotations), jnp.int32),
+            pltpu.SemaphoreType.DMA((3,)),
+        ],
         "forward",
     )(gate_angles, jnp.swapaxes(gate_pairs, 1, 2), x)
     z = exchange(send, AMP)
@@ -365,14 +368,15 @@
     )(hops, other, half4, half5, half6, hop_coef, hop_mask, u4_high, u4_low, z, gates)
     received = exchange(send, AMP)
     pack = ((5 * LANES, LANES), F32)
-    rows = ((5 * LANES // NEAR, LANES), F32)
-    adjoint, partial = call(backward_kernel, [((middle, LANES), F32), pack], [VMEM] * 10, [flat], "backward")(
+    far = devices // NEAR
+    rows = ((far * 5 * LANES // NEAR, LANES), F32)
+    adjoint, partial = call(backward_kernel, [((middle, LANES), F32, True), pack], [VMEM] * 10, [flat], "backward")(
         received, x_near, s1_high, s1_low, s2_high, s2_low, gates, k_high, k_low, upper
     )
-    (partial,) = call(near_sum_kernel, [rows], [VMEM], (), "near")(exchange(partial, "near"))
-    far_sum = functools.partial(far_sum_kernel, factor=2.0 / (devices * middle))
-    (sums,) = call(far_sum, [rows], [VMEM], (), "far")(exchange(partial, "far"))
-    (sums,) = call(hand_out_kernel, [pack], [VMEM], (), "hand")(exchange(sums, "far"))
+    near_sum = functools.partial(sum_and_copy_kernel, sources=NEAR, factor=1.0)
+    (partial,) = call(near_sum, [rows], [VMEM], (), "near")(exchange(partial, "near"))
+    far_sum = functools.partial(sum_and_copy_kernel, sources=far, factor=2.0 / (devices * middle))
+    (sums,) = call(far_sum, [pack], [VMEM], (), "far")(exchange(partial, "far"))
     (grads,) = call(gather_kernel, [((blocks, LANES, LANES), F32, True)], [VMEM], (), "gather")(exchange(sums, "near"))
     return adjoint.reshape(initial_state.shape), grads
 

time: 185 us -> 172 us (0.930)
  starting transfers between devices: 11.4 us -> 4.68 us
  waiting for transfers between devices: 11.2 us -> 4.84 us
  blocking collectives: 143 us -> 147 us
  local copies, waits for them, and re-layouts: 3.21 us -> 0.01 us
    all_to_all x1 -> x0, starting transfers between devices: 6.69 us -> none  [exchange(): lax.all_to_all(shaped, axes, split_axis=0, concat_axis=0, tiled=True)]
    all_to_all x1 -> x0, waiting for transfers between devices: 6.37 us -> none  [exchange(): lax.all_to_all(shaped, axes, split_axis=0, concat_axis=0, tiled=True)]
    all_to_all x5, blocking collectives: 143 us -> 147 us  [exchange(): lax.all_to_all(shaped, axes, split_axis=0, concat_axis=0, tiled=True)]
    unnamed x11 -> x4, local copies, waits for them, and re-layouts: 3.21 us -> 0.01 us
    pallas_call x9 -> x8, Pallas kernels: 14.7 us -> 15 us  [run(): return made(*kept)]
  transfers between devices with their start and end apart: 5 -> 4, of which waited for: 4 -> 3; matrix products, arithmetic and copies ran while one was open for 0% -> 0% of each run, Pallas kernels for 1% -> 1%
where the time goes in v3:
time: 172 us
  blocking collectives  147 us (85%)
  Pallas kernels  15 us (9%)
  waiting for transfers between devices  4.84 us (3%)
  starting transfers between devices  4.68 us (3%)
    all_to_all x5, blocking collectives, exchange(): lax.all_to_all(shaped, axes, split_axis=0, concat_axis=0, tiled=True)  147 us
    pallas_call x8, Pallas kernels, run(): return made(*kept)  15 us
    ppermute x4, waiting for transfers between devices, swapped(): lax.ppermute(value, AMP, [(i, i ^ flip) for i in range(lax.axis_size(AMP))])  4.84 us
    ppermute x4, starting transfers between devices, swapped(): lax.ppermute(value, AMP, [(i, i ^ flip) for i in range(lax.axis_size(AMP))])  4.68 us
  transfers between devices with their start and end apart: 4, of which 3 were waited for; matrix products, arithmetic and copies ran while one was open for 0% of the time, Pallas kernels for 1%

profile of v3, /device:TPU:33, one launch (start us, length us, event | category | flops | bytes accessed | tf_op | source)
XLA Modules:
  0.0 171.8 jit_solution(11358155645746098696)
XLA Ops:
  0.6 5.3 %forward.1 = (f32[1024,128]{1,0:T(8,128)S(1)}, f32[1024,128]{1,0:T(8,128)S(1)}, bf16[256,512]{1,0:T(8,128)(2,1)S(1)}, bf16[256,512]{1,0:T(8,128)(2,1)S(1)}, bf16...) custom-call(f32[5,16]{1,0:T(8,128)} %angles_far.1, ...), custom_call_target="tpu_custom_call" | custom-call | tf_op jit(solution)/shard_map/forward/pallas_call | solution.py:307
  5.9 61.5 %all_to_all.25 = f32[128,8,1,128]{3,1,2,0:T(8,128)S(1)} all-to-all(f32[128,8,1,128]{3,1,2,0:T(8,128)S(1)} %bitcast.32), channel_id=1, replica_groups=mesh['runs'=2,'far'=8,'near'=16] {'far','near'}, dimensions={0} | all-to-all | bytes 1048576 | tf_op jit(solution)/shard_map/all_to_all | solution.py:315
  67.5 0.9 turn.1
  68.3 0.6 collective-permute-start
  69.0 1.5 collective-permute-start.1
  70.5 0.0 copy-start
  70.5 0.0 copy-start.1
  70.5 2.1 %collective-permute-start.2 = (f32[64,1024]{1,0:T(8,128)S(1)}, f32[64,1024]{1,0:T(8,128)S(1)}, u32[]{:S(2)}, u32[]{:S(2)}) collective-permute-start(f32[64,1024]{1,0:T(8,128)S(1)} %get-tuple-element.25), channel_id=1, source_target_pairs={{0,6},{1,7},{2,4},{3,5},{4,2},{5,3},{6,0},{7,1},{8,14},{9,15},{10,... | collective-permute-start | bytes 786440 | tf_op jit(solution)/shard_map/ppermute | solution.py:319
  72.6 0.5 collective-permute-start.3
  73.0 0.0 copy-done
  73.0 0.0 copy-done.1
  73.0 1.9 %hops.1 = f32[128,1024]{1,0:T(8,128)S(1)} custom-call(f32[128,1024]{1,0:T(8,128)S(1)} %get-tuple-element.23.v, f32[23]{0:T(128)S(1)} %copy-done, s32[23]{0:T(128)S(1)} %copy-done.1), custom_call_target="tpu_custom_call" | custom-call | tf_op jit(solution)/shard_map/hops/pallas_call | solution.py:307
  74.9 1.9 %collective-permute-done.1.half4 = f32[64,1024]{1,0:T(8,128)S(1)} collective-permute-done((f32[64,1024]{1,0:T(8,128)S(1)}, f32[64,1024]{1,0:T(8,128)S(1)}, u32[]{:S(2)}, u32[]{:S(2)}) %collective-permute-start.1) | collective-permute-done | bytes 262176 | tf_op jit(solution)/shard_map/ppermute | solution.py:319
  76.8 2.1 %collective-permute-done.2.half5 = f32[64,1024]{1,0:T(8,128)S(1)} collective-permute-done((f32[64,1024]{1,0:T(8,128)S(1)}, f32[64,1024]{1,0:T(8,128)S(1)}, u32[]{:S(2)}, u32[]{:S(2)}) %collective-permute-start.2) | collective-permute-done | bytes 262176 | tf_op jit(solution)/shard_map/ppermute | solution.py:319
  78.9 0.8 collective-permute-done.3.half6
  79.7 0.0 collective-permute-done.other
  79.8 2.6 %back.1 = (f32[1024,128]{1,0:T(8,128)S(1)}, f32[2,128,128]{2,1,0:T(8,128)S(1)}) custom-call(f32[128,1024]{1,0:T(8,128)S(1)} %hops.1, f32[128,1024]{1,0:T(8,128)S(1)} %collective-permute-done.other, f32[64,1024]{1,0:T(8,128)S(1)} %collective-permute-done.1.half4, f32[64,1024]{1,0:T(8,128)S(1)} %collective-permute-done.2.half5, ...), custom_call_target="tpu_custom_call" | custom-call | tf_op jit(solution)/shard_map/back/pallas_call | solution.py:307
  82.4 40.2 %all_to_all.26 = f32[128,8,1,128]{3,1,2,0:T(8,128)S(1)} all-to-all(f32[128,8,1,128]{3,1,2,0:T(8,128)S(1)} %bitcast.31), channel_id=1, replica_groups=mesh['runs'=2,'far'=8,'near'=16] {'far','near'}, dimensions={0} | all-to-all | bytes 1048576 | tf_op jit(solution)/shard_map/all_to_all | solution.py:315
  122.6 3.6 %backward.1 = (f32[1024,128]{1,0:T(8,128)}, f32[640,128]{1,0:T(8,128)S(1)}) custom-call(f32[1024,128]{1,0:T(8,128)S(1)} %bitcast.25, f32[1024,128]{1,0:T(8,128)S(1)} %get-tuple-element.30.x, bf16[256,512]{1,0:T(8,128)(2,1)S(1)} %get-tuple-element.31.s1_high, bf16[256,512]{1,0:T(8,128)(2,1)S(1)} %get-tuple-element.32.s1_low, ...), custom_call_target="tpu_custom_call" | custom-call | tf_op jit(solution)/shard_map/backward/pallas_call | solution.py:307
  126.2 13.1 %all_to_all.27 = f32[16,40,1,128]{3,1,2,0:T(8,128)S(1)} all-to-all(f32[16,40,1,128]{3,1,2,0:T(8,128)S(1)} %bitcast.33), channel_id=1, replica_groups=mesh['runs'=2,'far'=8,'near'=16] {'near'}, dimensions={0} | all-to-all | bytes 655360 | tf_op jit(solution)/shard_map/all_to_all | solution.py:315
  139.3 16.9 %all_to_all.28 = f32[8,40,1,128]{3,1,2,0:T(8,128)S(1)} all-to-all(f32[8,40,1,128]{3,1,2,0:T(8,128)S(1)} %bitcast.29), channel_id=1, replica_groups=mesh['runs'=2,'far'=8,'near'=16] {'far'}, dimensions={0} | all-to-all | bytes 327680 | tf_op jit(solution)/shard_map/all_to_all | solution.py:315
  156.3 14.8 %all_to_all.29 = f32[16,40,1,128]{3,1,2,0:T(8,128)S(1)} all-to-all(f32[16,40,1,128]{3,1,2,0:T(8,128)S(1)} %bitcast.27), channel_id=1, replica_groups=mesh['runs'=2,'far'=8,'near'=16] {'near'}, dimensions={0} | all-to-all | bytes 655360 | tf_op jit(solution)/shard_map/all_to_all | solution.py:315
  171.0 0.7 gather.1
  (2 shorter events, 0.1 us)
Async XLA Ops:
  68.3 11.4 %collective-permute-start = (f32[128,1024]{1,0:T(8,128)S(1)}, f32[128,1024]{1,0:T(8,128)S(1)}, u32[]{:S(2)}, u32[]{:S(2)}) collective-permute-start(f32[128,1024]{1,0:T(8,128)S(1)} %get-tuple-element.23.v), channel_id=1, source_target_pairs={{0,1},{1,0},{2,3},{3,2},{4,5},{5,4},{6,7},{7,6},{8,9},{9,8},{10,11... | collective-permute-start | bytes 1572872 | tf_op jit(solution)/shard_map/ppermute | solution.py:319
  69.0 7.9 %collective-permute-start.1 = (f32[64,1024]{1,0:T(8,128)S(1)}, f32[64,1024]{1,0:T(8,128)S(1)}, u32[]{:S(2)}, u32[]{:S(2)}) collective-permute-start(f32[64,1024]{1,0:T(8,128)S(1)} %get-tuple-element.24), channel_id=1, source_target_pairs={{0,2},{1,3},{2,0},{3,1},{4,6},{5,7},{6,4},{7,5},{8,10},{9,11},{10,... | collective-permute-start | bytes 786440 | tf_op jit(solution)/shard_map/ppermute | solution.py:319
  70.5 2.6 %copy-start = (f32[23]{0:T(128)S(1)}, f32[23]{0:T(128)}, u32[]{:S(2)}) copy-start(f32[23]{0:T(128)} %coef.3) | copy-start | bytes 280
  70.5 2.6 %copy-start.1 = (s32[23]{0:T(128)S(1)}, s32[23]{0:T(128)}, u32[]{:S(2)}) copy-start(s32[23]{0:T(128)} %mask.3) | copy-start | bytes 280
  70.5 8.4 %collective-permute-start.2 = (f32[64,1024]{1,0:T(8,128)S(1)}, f32[64,1024]{1,0:T(8,128)S(1)}, u32[]{:S(2)}, u32[]{:S(2)}) collective-permute-start(f32[64,1024]{1,0:T(8,128)S(1)} %get-tuple-element.25), channel_id=1, source_target_pairs={{0,6},{1,7},{2,4},{3,5},{4,2},{5,3},{6,0},{7,1},{8,14},{9,15},{10,... | collective-permute-start | bytes 786440 | tf_op jit(solution)/shard_map/ppermute | solution.py:319
  72.6 7.2 %collective-permute-start.3 = (f32[64,1024]{1,0:T(8,128)S(1)}, f32[64,1024]{1,0:T(8,128)S(1)}, u32[]{:S(2)}, u32[]{:S(2)}) collective-permute-start(f32[64,1024]{1,0:T(8,128)S(1)} %get-tuple-element.26), channel_id=1, source_target_pairs={{0,8},{1,9},{2,10},{3,11},{4,12},{5,13},{6,14},{7,15},{8,0},{9,1},... | collective-permute-start | bytes 786440 | tf_op jit(solution)/shard_map/ppermute | solution.py:319

commit v4 on v3

--- a/solution.py
+++ b/solution.py
@@ -9,7 +9,7 @@
 from jax.sharding import PartitionSpec as P
 
 F32, BF16 = jnp.float32, jnp.bfloat16
-AMP = ("far", "near")
+AMP = ("far", "near", "core")
 VMEM = pl.BlockSpec(memory_space=pltpu.VMEM)
 SMEM = pl.BlockSpec(memory_space=pltpu.SMEM)
 FAR = pl.BlockSpec(memory_space=pltpu.HBM)
@@ -17,7 +17,8 @@
 LANES = 128
 LOW = 8
 PARTS = 4
-NEAR = 16
+CORES = 2
+NEAR = 8
 CHAIN_FIRST = 10
 RUNG_FIRST = 16
 
@@ -228,7 +229,9 @@
     grams[0] = gram
 
 
-def backward_kernel(received, x, s1_high, s1_low, s2_high, s2_low, gates, k_high, k_low, upper, adjoint, pack, nat):
+def backward_kernel(
+    received, x, s1_high, s1_low, s2_high, s2_low, gates, k_high, k_low, upper, lam1_high, lam1_low, own, away, nat, pack
+):
     for d in range(received.shape[0] // LOW):
         c = chunk_of(d)
         nat[c * LOW : (c + 1) * LOW, :] = received[d * LOW : (d + 1) * LOW, :]
@@ -253,18 +256,33 @@
     folded = dot(pick, high, dims) + dot(pick, low, dims)
     high, low = halves(folded)
     gram1 = jnp.dot(high, pick, preferred_element_type=F32) + jnp.dot(low, pick, preferred_element_type=F32)
-    lam1 = product(lam2, (k_high[...], k_low[...]), 1, 1)
-    g0 = gate(gates, 0)
+    lam1_high[...], lam1_low[...] = halves(product(lam2, (k_high[...], k_low[...]), 1, 1))
     gram0 = jnp.zeros((LANES, LANES), F32)
     for q in range(PARTS):
-        inner = halves(lam1[:, q * LANES : (q + 1) * LANES])
+        part = slice(q * LANES, (q + 1) * LANES)
+        inner = (lam1_high[:, part], lam1_low[:, part])
         gram0 = gram0 + product(inner, halves(x[pl.ds(q, count, stride=PARTS), :]), 0, 0)
-        adjoint[pl.ds(q, count, stride=PARTS), :] = product(inner, g0, 1, 1)
-    size = LANES // NEAR
-    total = 5 * size
+    size = LANES // (CORES * NEAR)
     for k, gram in enumerate((gram0, gram1, gram2, upper[0], upper[1])):
-        for d in range(NEAR):
-            pack[d * total + k * size : d * total + (k + 1) * size, :] = gram[d * size : (d + 1) * size, :]
+        for d in range(CORES * NEAR):
+            start = (d * 5 + k) * size
+            pack[start : start + size, :] = gram[d * size : (d + 1) * size, :]
+    core = own_bits()[0]
+    rows = own.shape[0]
+    own[...] = pack[pl.ds(pl.multiple_of(core * rows, rows), rows), :]
+    away[...] = pack[pl.ds(pl.multiple_of((1 - core) * rows, rows), rows), :]
+
+
+def finish_kernel(lam1_high, lam1_low, gates, adjoint):
+    g0 = gate(gates, 0)
+    count = lam1_high.shape[0]
+    for q in range(PARTS):
+        part = slice(q * LANES, (q + 1) * LANES)
+        adjoint[pl.ds(q, count, stride=PARTS), :] = product((lam1_high[:, part], lam1_low[:, part]), g0, 1, 1)
+
+
+def merge_kernel(own, other, merged):
+    merged[...] = own[...] + other[...]
 
 
 def sum_and_copy_kernel(received, pack, *, sources, factor):
@@ -276,12 +294,15 @@
         pack[d * size : (d + 1) * size, :] = factor * value
 
 
-def gather_kernel(received, grads):
-    size = LANES // NEAR
-    for d in range(NEAR):
-        for k in range(5):
-            start = (d * 5 + k) * size
-            grads[k, d * size : (d + 1) * size, :] = received[start : start + size, :]
+def gather_kernel(own, other, grads):
+    size = LANES // (CORES * NEAR)
+    core = own_bits()[0]
+    for source, half in ((own, core), (other, 1 - core)):
+        for d in range(NEAR):
+            row = pl.multiple_of((half * NEAR + d) * size, size)
+            for k in range(5):
+                start = (d * 5 + k) * size
+                grads[k, pl.ds(row, size), :] = source[start : start + size, :]
 
 
 def call(kernel, outs, specs, scratch=(), name=None):
@@ -356,8 +377,8 @@
         [flat],
         "turn",
     )(z, gates)
+    half4, half5, half6 = swapped(half4, 2), swapped(half5, 6), swapped(half6, 8)
     other = swapped(v, 1)
-    half4, half5, half6 = swapped(half4, 2), swapped(half5, 6), swapped(half6, 8)
     (hops,) = call(local_hops_kernel, [(turned, F32)], [VMEM, SMEM, SMEM], (), "hops")(v, hop_coef, hop_mask)
     send, upper = call(
         return_kernel,
@@ -367,23 +388,31 @@
         "back",
     )(hops, other, half4, half5, half6, hop_coef, hop_mask, u4_high, u4_low, z, gates)
     received = exchange(send, AMP)
-    pack = ((5 * LANES, LANES), F32)
-    far = devices // NEAR
-    rows = ((far * 5 * LANES // NEAR, LANES), F32)
-    adjoint, partial = call(backward_kernel, [((middle, LANES), F32, True), pack], [VMEM] * 10, [flat], "backward")(
-        received, x_near, s1_high, s1_low, s2_high, s2_low, gates, k_high, k_low, upper
-    )
+    part = ((5 * LANES // CORES, LANES), F32)
+    lam1_high, lam1_low, own, away = call(
+        backward_kernel,
+        [(wide, BF16), (wide, BF16), part, part],
+        [VMEM] * 10,
+        [flat, pltpu.VMEM((5 * LANES, LANES), F32)],
+        "backward",
+    )(received, x_near, s1_high, s1_low, s2_high, s2_low, gates, k_high, k_low, upper)
+    away = swapped(away, 1)
+    (adjoint,) = call(finish_kernel, [((middle, LANES), F32, True)], [VMEM] * 3, (), "finish")(lam1_high, lam1_low, gates)
+    (partial,) = call(merge_kernel, [part], [VMEM] * 2, (), "merge")(own, away)
+    far = devices // (CORES * NEAR)
+    rows = ((far * part[0][0] // NEAR, LANES), F32)
     near_sum = functools.partial(sum_and_copy_kernel, sources=NEAR, factor=1.0)
     (partial,) = call(near_sum, [rows], [VMEM], (), "near")(exchange(partial, "near"))
     far_sum = functools.partial(sum_and_copy_kernel, sources=far, factor=2.0 / (devices * middle))
-    (sums,) = call(far_sum, [pack], [VMEM], (), "far")(exchange(partial, "far"))
-    (grads,) = call(gather_kernel, [((blocks, LANES, LANES), F32, True)], [VMEM], (), "gather")(exchange(sums, "near"))
+    (sums,) = call(far_sum, [part], [VMEM], (), "far")(exchange(partial, "far"))
+    sums = exchange(sums, "near")
+    (grads,) = call(gather_kernel, [((blocks, LANES, LANES), F32, True)], [VMEM] * 2, (), "gather")(sums, swapped(sums, 1))
     return adjoint.reshape(initial_state.shape), grads
 
 
 def solution(mesh):
     runs, amp = mesh.shape["runs"], mesh.shape["amp"]
-    split = Mesh(mesh.devices.reshape(runs, amp // NEAR, NEAR), ("runs",) + AMP)
+    split = Mesh(mesh.devices.reshape(runs, amp // (NEAR * CORES), NEAR, CORES), ("runs",) + AMP)
     return jax.shard_map(
         on_device,
         mesh=split,

time: 172 us -> 170 us (0.988)
  blocking collectives: 147 us -> 137 us
  starting transfers between devices: 4.68 us -> 10.4 us
    all_to_all x5, blocking collectives: 147 us -> 137 us  [exchange(): lax.all_to_all(shaped, axes, split_axis=0, concat_axis=0, tiled=True)]
    ppermute x4 -> x6, starting transfers between devices: 4.68 us -> 10.4 us  [swapped(): lax.ppermute(value, AMP, [(i, i ^ flip) for i in range(lax.axis_size(AMP))])]
    ppermute x4 -> x6, waiting for transfers between devices: 4.84 us -> 5.86 us  [swapped(): lax.ppermute(value, AMP, [(i, i ^ flip) for i in range(lax.axis_size(AMP))])]
    pallas_call x8 -> x10, Pallas kernels: 15 us -> 15.4 us  [run(): return made(*kept)]
  transfers between devices with their start and end apart: 4 -> 6, of which waited for: 3 -> 4; matrix products, arithmetic and copies ran while one was open for 0% -> 0% of each run, Pallas kernels for 1% -> 2%
where the time goes in v4:
time: 170 us; the launch traced here: 169 us
  blocking collectives  137 us (81%)
  Pallas kernels  15.4 us (9%)
  starting transfers between devices  10.4 us (6%)
  waiting for transfers between devices  5.86 us (3%)
    all_to_all x5, blocking collectives, exchange(): lax.all_to_all(shaped, axes, split_axis=0, concat_axis=0, tiled=True)  137 us
    pallas_call x10, Pallas kernels, run(): return made(*kept)  15.4 us
    ppermute x6, starting transfers between devices, swapped(): lax.ppermute(value, AMP, [(i, i ^ flip) for i in range(lax.axis_size(AMP))])  10.4 us
    ppermute x6, waiting for transfers between devices, swapped(): lax.ppermute(value, AMP, [(i, i ^ flip) for i in range(lax.axis_size(AMP))])  5.86 us
  transfers between devices with their start and end apart: 6, of which 4 were waited for; matrix products, arithmetic and copies ran while one was open for 0% of the time, Pallas kernels for 2%

profile of v4, /device:TPU:33, one launch (start us, length us, event | category | flops | bytes accessed | tf_op | source)
XLA Modules:
  0.0 169.5 jit_solution(15609871898463825020)
XLA Ops:
  0.6 5.3 %forward.1 = (f32[1024,128]{1,0:T(8,128)S(1)}, f32[1024,128]{1,0:T(8,128)S(1)}, bf16[256,512]{1,0:T(8,128)(2,1)S(1)}, bf16[256,512]{1,0:T(8,128)(2,1)S(1)}, bf16...) custom-call(f32[5,16]{1,0:T(8,128)} %angles_far.1, ...), custom_call_target="tpu_custom_call" | custom-call | tf_op jit(solution)/shard_map/forward/pallas_call | solution.py:328
  5.9 61.5 %all_to_all.25 = f32[128,8,1,128]{3,1,2,0:T(8,128)S(1)} all-to-all(f32[128,8,1,128]{3,1,2,0:T(8,128)S(1)} %bitcast.34), channel_id=1, replica_groups=mesh['runs'=2,'far'=8,'near'=8,'core'=2] {'far','near','core'}, dimensions={0} | all-to-all | bytes 1048576 | tf_op jit(solution)/shard_map/all_to_all | solution.py:336
  67.5 0.9 turn.1
  68.4 0.6 collective-permute-start
  69.0 1.5 collective-permute-start.1
  70.5 0.0 copy-start
  70.5 0.0 copy-start.1
  70.5 2.1 %collective-permute-start.2 = (f32[64,1024]{1,0:T(8,128)S(1)}, f32[64,1024]{1,0:T(8,128)S(1)}, u32[]{:S(2)}, u32[]{:S(2)}) collective-permute-start(f32[64,1024]{1,0:T(8,128)S(1)} %get-tuple-element.27), channel_id=1, source_target_pairs={{0,6},{1,7},{2,4},{3,5},{4,2},{5,3},{6,0},{7,1},{8,14},{9,15},{10,... | collective-permute-start | bytes 786440 | tf_op jit(solution)/shard_map/ppermute | solution.py:340
  72.6 0.5 collective-permute-start.3
  73.0 0.0 copy-done
  73.0 0.0 copy-done.1
  73.1 1.9 %hops.1 = f32[128,1024]{1,0:T(8,128)S(1)} custom-call(f32[128,1024]{1,0:T(8,128)S(1)} %get-tuple-element.25.v, f32[23]{0:T(128)S(1)} %copy-done, s32[23]{0:T(128)S(1)} %copy-done.1), custom_call_target="tpu_custom_call" | custom-call | tf_op jit(solution)/shard_map/hops/pallas_call | solution.py:328
  74.9 1.9 %collective-permute-done.1.half4 = f32[64,1024]{1,0:T(8,128)S(1)} collective-permute-done((f32[64,1024]{1,0:T(8,128)S(1)}, f32[64,1024]{1,0:T(8,128)S(1)}, u32[]{:S(2)}, u32[]{:S(2)}) %collective-permute-start.1) | collective-permute-done | bytes 262176 | tf_op jit(solution)/shard_map/ppermute | solution.py:340
  76.9 2.1 %collective-permute-done.2.half5 = f32[64,1024]{1,0:T(8,128)S(1)} collective-permute-done((f32[64,1024]{1,0:T(8,128)S(1)}, f32[64,1024]{1,0:T(8,128)S(1)}, u32[]{:S(2)}, u32[]{:S(2)}) %collective-permute-start.2) | collective-permute-done | bytes 262176 | tf_op jit(solution)/shard_map/ppermute | solution.py:340
  78.9 0.8 collective-permute-done.3.half6
  79.8 0.0 collective-permute-done.other
  79.8 2.6 %back.1 = (f32[1024,128]{1,0:T(8,128)S(1)}, f32[2,128,128]{2,1,0:T(8,128)S(1)}) custom-call(f32[128,1024]{1,0:T(8,128)S(1)} %hops.1, f32[128,1024]{1,0:T(8,128)S(1)} %collective-permute-done.other, f32[64,1024]{1,0:T(8,128)S(1)} %collective-permute-done.1.half4, f32[64,1024]{1,0:T(8,128)S(1)} %collective-permute-done.2.half5, ...), custom_call_target="tpu_custom_call" | custom-call | tf_op jit(solution)/shard_map/back/pallas_call | solution.py:328
  82.4 40.2 %all_to_all.26 = f32[128,8,1,128]{3,1,2,0:T(8,128)S(1)} all-to-all(f32[128,8,1,128]{3,1,2,0:T(8,128)S(1)} %bitcast.33), channel_id=1, replica_groups=mesh['runs'=2,'far'=8,'near'=8,'core'=2] {'far','near','core'}, dimensions={0} | all-to-all | bytes 1048576 | tf_op jit(solution)/shard_map/all_to_all | solution.py:336
  122.6 2.7 %backward.1 = (bf16[256,512]{1,0:T(8,128)(2,1)S(1)}, bf16[256,512]{1,0:T(8,128)(2,1)S(1)}, f32[320,128]{1,0:T(8,128)S(1)}, f32[320,128]{1,0:T(8,128)S(1)}) custom-call(f32[1024,128]{1,0:T(8,128)S(1)} %bitcast.25, f32[1024,128]{1,0:T(8,128)S(1)} %get-tuple-element.32.x, bf16[256,512]{1,0:T(8,128)(2,1)S(1)} %get-tuple-element.33.s1_high, ...), custom_call_target="tpu_custom_call" | custom-call | tf_op jit(solution)/shard_map/backward/pallas_call | solution.py:328
  125.4 0.6 collective-permute-start.4
  126.0 1.0 collective-permute-done.4.other
  127.0 10.6 %all_to_all.27 = f32[8,40,1,128]{3,1,2,0:T(8,128)S(1)} all-to-all(f32[8,40,1,128]{3,1,2,0:T(8,128)S(1)} %bitcast.32), channel_id=1, replica_groups=mesh['runs'=2,'far'=8,'near'=8,'core'=2] {'near'}, dimensions={0} | all-to-all | bytes 327680 | tf_op jit(solution)/shard_map/all_to_all | solution.py:336
  137.6 16.7 %all_to_all.28 = f32[8,40,1,128]{3,1,2,0:T(8,128)S(1)} all-to-all(f32[8,40,1,128]{3,1,2,0:T(8,128)S(1)} %bitcast.29), channel_id=1, replica_groups=mesh['runs'=2,'far'=8,'near'=8,'core'=2] {'far'}, dimensions={0} | all-to-all | bytes 327680 | tf_op jit(solution)/shard_map/all_to_all | solution.py:336
  154.3 8.1 %all_to_all.29 = f32[8,40,1,128]{3,1,2,0:T(8,128)S(1)} all-to-all(f32[8,40,1,128]{3,1,2,0:T(8,128)S(1)} %bitcast.31), channel_id=1, replica_groups=mesh['runs'=2,'far'=8,'near'=8,'core'=2] {'near'}, dimensions={0} | all-to-all | bytes 327680 | tf_op jit(solution)/shard_map/all_to_all | solution.py:336
  162.5 5.1 %collective-permute-start.5 = (f32[320,128]{1,0:T(8,128)S(1)}, f32[320,128]{1,0:T(8,128)S(1)}, u32[]{:S(2)}, u32[]{:S(2)}) collective-permute-start(f32[320,128]{1,0:T(8,128)S(1)} %bitcast.26), channel_id=1, source_target_pairs={{0,1},{1,0},{2,3},{3,2},{4,5},{5,4},{6,7},{7,6},{8,9},{9,8},{10,11... | collective-permute-start | bytes 491528 | tf_op jit(solution)/shard_map/ppermute | solution.py:340
  167.5 1.2 finish.1
  168.7 0.0 collective-permute-done.5.other
  168.7 0.8 gather.1
  (3 shorter events, 0.1 us)
Async XLA Ops:
  68.4 11.4 %collective-permute-start = (f32[128,1024]{1,0:T(8,128)S(1)}, f32[128,1024]{1,0:T(8,128)S(1)}, u32[]{:S(2)}, u32[]{:S(2)}) collective-permute-start(f32[128,1024]{1,0:T(8,128)S(1)} %get-tuple-element.25.v), channel_id=1, source_target_pairs={{0,1},{1,0},{2,3},{3,2},{4,5},{5,4},{6,7},{7,6},{8,9},{9,8},{10,11... | collective-permute-start | bytes 1572872 | tf_op jit(solution)/shard_map/ppermute | solution.py:340
  69.0 7.9 %collective-permute-start.1 = (f32[64,1024]{1,0:T(8,128)S(1)}, f32[64,1024]{1,0:T(8,128)S(1)}, u32[]{:S(2)}, u32[]{:S(2)}) collective-permute-start(f32[64,1024]{1,0:T(8,128)S(1)} %get-tuple-element.26), channel_id=1, source_target_pairs={{0,2},{1,3},{2,0},{3,1},{4,6},{5,7},{6,4},{7,5},{8,10},{9,11},{10,... | collective-permute-start | bytes 786440 | tf_op jit(solution)/shard_map/ppermute | solution.py:340
  70.5 2.5 %copy-start = (f32[23]{0:T(128)S(1)}, f32[23]{0:T(128)}, u32[]{:S(2)}) copy-start(f32[23]{0:T(128)} %coef.3) | copy-start | bytes 280
  70.5 2.5 %copy-start.1 = (s32[23]{0:T(128)S(1)}, s32[23]{0:T(128)}, u32[]{:S(2)}) copy-start(s32[23]{0:T(128)} %mask.3) | copy-start | bytes 280
  70.5 8.4 %collective-permute-start.2 = (f32[64,1024]{1,0:T(8,128)S(1)}, f32[64,1024]{1,0:T(8,128)S(1)}, u32[]{:S(2)}, u32[]{:S(2)}) collective-permute-start(f32[64,1024]{1,0:T(8,128)S(1)} %get-tuple-element.27), channel_id=1, source_target_pairs={{0,6},{1,7},{2,4},{3,5},{4,2},{5,3},{6,0},{7,1},{8,14},{9,15},{10,... | collective-permute-start | bytes 786440 | tf_op jit(solution)/shard_map/ppermute | solution.py:340
  72.6 7.2 %collective-permute-start.3 = (f32[64,1024]{1,0:T(8,128)S(1)}, f32[64,1024]{1,0:T(8,128)S(1)}, u32[]{:S(2)}, u32[]{:S(2)}) collective-permute-start(f32[64,1024]{1,0:T(8,128)S(1)} %get-tuple-element.28), channel_id=1, source_target_pairs={{0,8},{1,9},{2,10},{3,11},{4,12},{5,13},{6,14},{7,15},{8,0},{9,1},... | collective-permute-start | bytes 786440 | tf_op jit(solution)/shard_map/ppermute | solution.py:340
  125.4 1.6 collective-permute-start.4
  162.5 6.3 %collective-permute-start.5 = (f32[320,128]{1,0:T(8,128)S(1)}, f32[320,128]{1,0:T(8,128)S(1)}, u32[]{:S(2)}, u32[]{:S(2)}) collective-permute-start(f32[320,128]{1,0:T(8,128)S(1)} %bitcast.26), channel_id=1, source_target_pairs={{0,1},{1,0},{2,3},{3,2},{4,5},{5,4},{6,7},{7,6},{8,9},{9,8},{10,11... | collective-permute-start | bytes 491528 | tf_op jit(solution)/shard_map/ppermute | solution.py:340

commit v5 on v4

--- a/solution.py
+++ b/solution.py
@@ -19,6 +19,8 @@
 PARTS = 4
 CORES = 2
 NEAR = 8
+GROUP = LANES // PARTS
+LANE_BIT = (5, 6, 0, 1, 2, 3, 4)
 CHAIN_FIRST = 10
 RUNG_FIRST = 16
 
@@ -33,9 +35,10 @@
 
 
 def product(left, right, left_dim, right_dim):
+    lefts = jnp.concatenate([left[0], left[0], left[1]], axis=left_dim)
+    rights = jnp.concatenate([right[0], right[1], right[0]], axis=right_dim)
     dims = (((left_dim,), (right_dim,)), ((), ()))
-    dot = lambda a, b: lax.dot_general(a, b, dims, preferred_element_type=F32)
-    return dot(left[0], right[0]) + (dot(left[0], right[1]) + dot(left[1], right[0]))
+    return lax.dot_general(lefts, rights, dims, preferred_element_type=F32)
 
 
 def own_bits():
@@ -43,21 +46,31 @@
     return [(chunk >> k) & 1 for k in range(4)]
 
 
-def spread_selector():
-    rows = lax.broadcasted_iota(jnp.int32, (PARTS * LANES, LANES), 0)
-    columns = lax.broadcasted_iota(jnp.int32, (PARTS * LANES, LANES), 1)
-    return ((rows >> 2) == columns).astype(F32).astype(BF16)
-
-
-def same_part():
-    shape = (PARTS * LANES, PARTS * LANES)
-    rows = lax.broadcasted_iota(jnp.int32, shape, 0)
-    columns = lax.broadcasted_iota(jnp.int32, shape, 1)
-    return ((rows ^ columns) & (PARTS - 1)) == 0
+def lane_order():
+    rows = lax.broadcasted_iota(jnp.int32, (LANES, LANES), 0)
+    lanes = lax.broadcasted_iota(jnp.int32, (LANES, LANES), 1)
+    return (lanes == (rows & (PARTS - 1)) * GROUP + (rows >> 2)).astype(F32).astype(BF16)
+
+
+def regroup(blocks):
+    group = lax.broadcasted_iota(jnp.int32, blocks[0].shape, 1) // GROUP
+    made = []
+    for w in range(PARTS):
+        total = None
+        for u in range(PARTS):
+            shift = (u - w) * GROUP % LANES
+            moved = pltpu.roll(blocks[u], shift, 1) if shift else blocks[u]
+            total = moved if total is None else jnp.where(group == u, moved, total)
+        made.append(total)
+    return made
+
+
+def columns_of(array, number):
+    return array[:, number * LANES : (number + 1) * LANES]
 
 
 def forward_kernel(
-    angles_far, pairs_far, x_far, send, x, s1_high, s1_low, s2_high, s2_low, gates, k_high, k_low,
+    angles_far, pairs_far, x_far, send, x, s1_high, s1_low, s2_high, s2_low, gates,
     level_high, level_low, nat, angles, pairs, arrived,
 ):
     small = [
@@ -116,25 +129,24 @@
                 else:
                     gates[b], gates[block_count + b] = high, low
 
-    pick = spread_selector()
-    keep = same_part()
-    for out, source in ((k_high, gates[1]), (k_low, gates[block_count + 1])):
-        spread = jnp.dot(pick, source, preferred_element_type=F32).astype(BF16)
-        wide = lax.dot_general(spread, pick, (((1,), (1,)), ((), ())), preferred_element_type=F32)
-        out[...] = jnp.where(keep, wide, 0.0).astype(BF16)
+    order = lane_order()
+    for slot in (0, block_count):
+        gates[slot] = jnp.dot(gates[slot], order, preferred_element_type=F32).astype(BF16)
     load.wait()
     g0 = gate(gates, 0)
-    for q in range(PARTS):
-        part = x[pl.ds(q, x.shape[0] // PARTS, stride=PARTS), :]
-        columns = slice(q * LANES, (q + 1) * LANES)
-        s1_high[:, columns], s1_low[:, columns] = halves(product(halves(part), g0, 1, 0))
-    s2_high[...], s2_low[...] = halves(product((s1_high[...], s1_low[...]), (k_high[...], k_low[...]), 1, 0))
+    parts = [halves(x[pl.ds(q, x.shape[0] // PARTS, stride=PARTS), :]) for q in range(PARTS)]
+    g1 = gate(gates, 1)
+    for number, block in enumerate(regroup([product(part, g0, 1, 0) for part in parts])):
+        columns = slice(number * LANES, (number + 1) * LANES)
+        high, low = halves(block)
+        s1_high[:, columns], s1_low[:, columns] = high, low
+        s2_high[:, columns], s2_low[:, columns] = halves(product((high, low), g1, 1, 0))
     g2 = gate(gates, 2)
     for e in range(s2_high.shape[0] // LANES):
         rows = slice(e * LANES, (e + 1) * LANES)
         s3 = product(g2, (s2_high[rows, :], s2_low[rows, :]), 0, 0)
-        for q in range(PARTS):
-            nat[pl.ds(e * PARTS * LANES + q, LANES, stride=PARTS), :] = s3[:, q * LANES : (q + 1) * LANES]
+        for p, block in enumerate(regroup([columns_of(s3, number) for number in range(PARTS)])):
+            nat[pl.ds(e * PARTS * LANES + p, LANES, stride=PARTS), :] = block
     for d in range(send.shape[0] // LOW):
         c = chunk_of(d)
         send[d * LOW : (d + 1) * LOW, :] = nat[c * LOW : (c + 1) * LOW, :]
@@ -173,7 +185,7 @@
 
 
 def local_hops_kernel(v, coef, mask, out):
-    lane_chain = sum(pair_matrix(k, k + 1, weight(coef, mask, k)) for k in range(6))
+    lane_chain = sum(pair_matrix(LANE_BIT[k], LANE_BIT[k + 1], weight(coef, mask, k)) for k in range(6))
     top_chain = sum(pair_matrix(k, k + 1, weight(coef, mask, CHAIN_FIRST + k)) for k in range(6))
     lane_chain, top_chain = halves(lane_chain), halves(top_chain)
     rows = lax.broadcasted_iota(jnp.int32, (LANES, LANES), 0)
@@ -189,8 +201,9 @@
         total = product(parts[c], lane_chain, 1, 0) + product(top_chain, parts[c], 1, 0)
         for k in range(3):
             total = total + product(rungs[k][(c >> k) & 1], parts[c ^ (1 << k)], 1, 0)
-        moved = pltpu.roll(blocks[c ^ 1], LANES // 2, 1)
-        wanted = (columns >> 6) == 1 - (c & 1)
+        step = 1 << LANE_BIT[6]
+        moved = pltpu.roll(blocks[c ^ 1], LANES - step if c & 1 else step, 1)
+        wanted = ((columns >> LANE_BIT[6]) & 1) == 1 - (c & 1)
         total = total + jnp.where(wanted, weight(coef, mask, 6) * moved, 0.0)
         for k in range(2):
             if (c >> k) & 1 != (c >> (k + 1)) & 1:
@@ -230,7 +243,7 @@
 
 
 def backward_kernel(
-    received, x, s1_high, s1_low, s2_high, s2_low, gates, k_high, k_low, upper, lam1_high, lam1_low, own, away, nat, pack
+    received, x, s1_high, s1_low, s2_high, s2_low, gates, upper, lam1_high, lam1_low, own, away, nat, pack
 ):
     for d in range(received.shape[0] // LOW):
         c = chunk_of(d)
@@ -241,27 +254,28 @@
     pieces = []
     for e in range(count // LANES):
         rows = slice(e * LANES, (e + 1) * LANES)
-        lam3 = jnp.concatenate(
-            [nat[pl.ds(e * PARTS * LANES + q, LANES, stride=PARTS), :] for q in range(PARTS)], axis=1
-        )
-        lam3 = halves(lam3)
+        blocks = [nat[pl.ds(e * PARTS * LANES + p, LANES, stride=PARTS), :] for p in range(PARTS)]
+        lam3 = halves(jnp.concatenate(regroup(blocks), axis=1))
         gram2 = gram2 + product(lam3, (s2_high[rows, :], s2_low[rows, :]), 1, 1)
         pieces.append(product(g2, lam3, 1, 0))
     lam2 = halves(jnp.concatenate(pieces, axis=0))
-    wide = jnp.where(same_part(), product(lam2, (s1_high[...], s1_low[...]), 0, 0), 0.0)
-    pick = spread_selector()
-    dims = (((0,), (0,)), ((), ()))
-    high, low = halves(wide)
-    dot = functools.partial(lax.dot_general, preferred_element_type=F32)
-    folded = dot(pick, high, dims) + dot(pick, low, dims)
-    high, low = halves(folded)
-    gram1 = jnp.dot(high, pick, preferred_element_type=F32) + jnp.dot(low, pick, preferred_element_type=F32)
-    lam1_high[...], lam1_low[...] = halves(product(lam2, (k_high[...], k_low[...]), 1, 1))
+    g1 = gate(gates, 1)
+    gram1 = jnp.zeros((LANES, LANES), F32)
+    blocks = []
+    for number in range(PARTS):
+        inner = (columns_of(lam2[0], number), columns_of(lam2[1], number))
+        gram1 = gram1 + product(inner, (columns_of(s1_high, number), columns_of(s1_low, number)), 0, 0)
+        blocks.append(product(inner, g1, 1, 1))
     gram0 = jnp.zeros((LANES, LANES), F32)
-    for q in range(PARTS):
-        part = slice(q * LANES, (q + 1) * LANES)
-        inner = (lam1_high[:, part], lam1_low[:, part])
+    for q, block in enumerate(regroup(blocks)):
+        columns = slice(q * LANES, (q + 1) * LANES)
+        inner = halves(block)
+        lam1_high[:, columns], lam1_low[:, columns] = inner
         gram0 = gram0 + product(inner, halves(x[pl.ds(q, count, stride=PARTS), :]), 0, 0)
+    order = lane_order()
+    dot = functools.partial(jnp.dot, preferred_element_type=F32)
+    high, low = halves(gram0)
+    gram0 = dot(order, high) + dot(order, low)
     size = LANES // (CORES * NEAR)
     for k, gram in enumerate((gram0, gram1, gram2, upper[0], upper[1])):
         for d in range(CORES * NEAR):
@@ -273,7 +287,8 @@
     away[...] = pack[pl.ds(pl.multiple_of((1 - core) * rows, rows), rows), :]
 
 
-def finish_kernel(lam1_high, lam1_low, gates, adjoint):
+def finish_kernel(lam1_high, lam1_low, gates, adjoint, done):
+    done[...] = jnp.zeros_like(done)
     g0 = gate(gates, 0)
     count = lam1_high.shape[0]
     for q in range(PARTS):
@@ -281,7 +296,7 @@
         adjoint[pl.ds(q, count, stride=PARTS), :] = product((lam1_high[:, part], lam1_low[:, part]), g0, 1, 1)
 
 
-def merge_kernel(own, other, merged):
+def merge_kernel(own, other, done, merged):
     merged[...] = own[...] + other[...]
 
 
@@ -348,16 +363,14 @@
     wide = (middle // PARTS, PARTS * LANES)
     turned = (devices, LOW * LANES)
     half = (devices // 2, LOW * LANES)
-    square = (PARTS * LANES, PARTS * LANES)
     level = pltpu.VMEM((blocks, rotations // 2, LANES, LANES), BF16)
     flat = pltpu.VMEM((middle, LANES), F32)
 
-    send, x_near, s1_high, s1_low, s2_high, s2_low, gates, k_high, k_low = call(
+    send, x_near, s1_high, s1_low, s2_high, s2_low, gates = call(
         forward_kernel,
         [((middle, LANES), F32)] * 2
         + [(wide, BF16)] * 4
-        + [((2 * blocks, LANES, LANES), BF16)]
-        + [(square, BF16)] * 2,
+        + [((2 * blocks, LANES, LANES), BF16)],
         [FAR] * 3,
         [
             level,
@@ -392,13 +405,15 @@
     lam1_high, lam1_low, own, away = call(
         backward_kernel,
         [(wide, BF16), (wide, BF16), part, part],
-        [VMEM] * 10,
+        [VMEM] * 8,
         [flat, pltpu.VMEM((5 * LANES, LANES), F32)],
         "backward",
-    )(received, x_near, s1_high, s1_low, s2_high, s2_low, gates, k_high, k_low, upper)
+    )(received, x_near, s1_high, s1_low, s2_high, s2_low, gates, upper)
     away = swapped(away, 1)
-    (adjoint,) = call(finish_kernel, [((middle, LANES), F32, True)], [VMEM] * 3, (), "finish")(lam1_high, lam1_low, gates)
-    (partial,) = call(merge_kernel, [part], [VMEM] * 2, (), "merge")(own, away)
+    adjoint, done = call(
+        finish_kernel, [((middle, LANES), F32, True), ((LOW, LANES), F32)], [VMEM] * 3, (), "finish"
+    )(lam1_high, lam1_low, gates)
+    (partial,) = call(merge_kernel, [part], [VMEM] * 3, (), "merge")(own, away, done)
     far = devices // (CORES * NEAR)
     rows = ((far * part[0][0] // NEAR, LANES), F32)
     near_sum = functools.partial(sum_and_copy_kernel, sources=NEAR, factor=1.0)

time: 170 us -> 169 us (level)
  no operation moved by 1% of the time
where the time goes in v5:
time: 169 us; the launch traced here: 168 us
  blocking collectives  138 us (82%)
  Pallas kernels  13.9 us (8%)
  starting transfers between devices  9.69 us (6%)
  waiting for transfers between devices  5.87 us (3%)
    all_to_all x5, blocking collectives, exchange(): lax.all_to_all(shaped, axes, split_axis=0, concat_axis=0, tiled=True)  138 us
    pallas_call x10, Pallas kernels, run(): return made(*kept)  13.9 us
    ppermute x6, starting transfers between devices, swapped(): lax.ppermute(value, AMP, [(i, i ^ flip) for i in range(lax.axis_size(AMP))])  9.69 us
    ppermute x6, waiting for transfers between devices, swapped(): lax.ppermute(value, AMP, [(i, i ^ flip) for i in range(lax.axis_size(AMP))])  5.87 us
  transfers between devices with their start and end apart: 6, of which 4 were waited for; matrix products, arithmetic and copies ran while one was open for 0% of the time, Pallas kernels for 2%

profile of v5, /device:TPU:33, one launch (start us, length us, event | category | flops | bytes accessed | tf_op | source)
XLA Modules:
  0.0 168.4 jit_solution(12398532291171226893)
XLA Ops:
  0.6 5.2 %forward.1 = (f32[1024,128]{1,0:T(8,128)S(1)}, f32[1024,128]{1,0:T(8,128)S(1)}, bf16[256,512]{1,0:T(8,128)(2,1)S(1)}, bf16[256,512]{1,0:T(8,128)(2,1)S(1)}, bf16...) custom-call(f32[5,16]{1,0:T(8,128)} %angles_far.1, ...), custom_call_target="tpu_custom_call" | custom-call | tf_op jit(solution)/shard_map/forward/pallas_call | solution.py:343
  5.8 61.5 %all_to_all.25 = f32[128,8,1,128]{3,1,2,0:T(8,128)S(1)} all-to-all(f32[128,8,1,128]{3,1,2,0:T(8,128)S(1)} %bitcast.34), channel_id=1, replica_groups=mesh['runs'=2,'far'=8,'near'=8,'core'=2] {'far','near','core'}, dimensions={0} | all-to-all | bytes 1048576 | tf_op jit(solution)/shard_map/all_to_all | solution.py:351
  67.4 0.8 turn.1
  68.2 0.6 collective-permute-start
  68.8 1.5 collective-permute-start.1
  70.3 0.0 copy-start
  70.3 0.0 copy-start.1
  70.3 2.1 %collective-permute-start.2 = (f32[64,1024]{1,0:T(8,128)S(1)}, f32[64,1024]{1,0:T(8,128)S(1)}, u32[]{:S(2)}, u32[]{:S(2)}) collective-permute-start(f32[64,1024]{1,0:T(8,128)S(1)} %get-tuple-element.27), channel_id=1, source_target_pairs={{0,6},{1,7},{2,4},{3,5},{4,2},{5,3},{6,0},{7,1},{8,14},{9,15},{10,... | collective-permute-start | bytes 786440 | tf_op jit(solution)/shard_map/ppermute | solution.py:355
  72.4 0.5 collective-permute-start.3
  72.9 0.0 copy-done
  72.9 0.0 copy-done.1
  72.9 1.9 %hops.1 = f32[128,1024]{1,0:T(8,128)S(1)} custom-call(f32[128,1024]{1,0:T(8,128)S(1)} %get-tuple-element.25.v, f32[23]{0:T(128)S(1)} %copy-done, s32[23]{0:T(128)S(1)} %copy-done.1), custom_call_target="tpu_custom_call" | custom-call | tf_op jit(solution)/shard_map/hops/pallas_call | solution.py:343
  74.7 1.9 %collective-permute-done.1.half4 = f32[64,1024]{1,0:T(8,128)S(1)} collective-permute-done((f32[64,1024]{1,0:T(8,128)S(1)}, f32[64,1024]{1,0:T(8,128)S(1)}, u32[]{:S(2)}, u32[]{:S(2)}) %collective-permute-start.1) | collective-permute-done | bytes 262176 | tf_op jit(solution)/shard_map/ppermute | solution.py:355
  76.7 2.1 %collective-permute-done.2.half5 = f32[64,1024]{1,0:T(8,128)S(1)} collective-permute-done((f32[64,1024]{1,0:T(8,128)S(1)}, f32[64,1024]{1,0:T(8,128)S(1)}, u32[]{:S(2)}, u32[]{:S(2)}) %collective-permute-start.2) | collective-permute-done | bytes 262176 | tf_op jit(solution)/shard_map/ppermute | solution.py:355
  78.8 0.8 collective-permute-done.3.half6
  79.6 0.0 collective-permute-done.other
  79.6 2.0 %back.1 = (f32[1024,128]{1,0:T(8,128)S(1)}, f32[2,128,128]{2,1,0:T(8,128)S(1)}) custom-call(f32[128,1024]{1,0:T(8,128)S(1)} %hops.1, f32[128,1024]{1,0:T(8,128)S(1)} %collective-permute-done.other, f32[64,1024]{1,0:T(8,128)S(1)} %collective-permute-done.1.half4, f32[64,1024]{1,0:T(8,128)S(1)} %collective-permute-done.2.half5, ...), custom_call_target="tpu_custom_call" | custom-call | tf_op jit(solution)/shard_map/back/pallas_call | solution.py:343
  81.6 40.2 %all_to_all.26 = f32[128,8,1,128]{3,1,2,0:T(8,128)S(1)} all-to-all(f32[128,8,1,128]{3,1,2,0:T(8,128)S(1)} %bitcast.33), channel_id=1, replica_groups=mesh['runs'=2,'far'=8,'near'=8,'core'=2] {'far','near','core'}, dimensions={0} | all-to-all | bytes 1048576 | tf_op jit(solution)/shard_map/all_to_all | solution.py:351
  121.8 2.0 %backward.1 = (bf16[256,512]{1,0:T(8,128)(2,1)S(1)}, bf16[256,512]{1,0:T(8,128)(2,1)S(1)}, f32[320,128]{1,0:T(8,128)S(1)}, f32[320,128]{1,0:T(8,128)S(1)}) custom-call(f32[1024,128]{1,0:T(8,128)S(1)} %bitcast.25, f32[1024,128]{1,0:T(8,128)S(1)} %get-tuple-element.32.x, bf16[256,512]{1,0:T(8,128)(2,1)S(1)} %get-tuple-element.33.s1_high, ...), custom_call_target="tpu_custom_call" | custom-call | tf_op jit(solution)/shard_map/backward/pallas_call | solution.py:343
  123.8 0.6 collective-permute-start.4
  124.4 1.2 finish.1
  125.6 0.0 collective-permute-done.4.other
  125.6 10.6 %all_to_all.27 = f32[8,40,1,128]{3,1,2,0:T(8,128)S(1)} all-to-all(f32[8,40,1,128]{3,1,2,0:T(8,128)S(1)} %bitcast.28), channel_id=1, replica_groups=mesh['runs'=2,'far'=8,'near'=8,'core'=2] {'near'}, dimensions={0} | all-to-all | bytes 327680 | tf_op jit(solution)/shard_map/all_to_all | solution.py:351
  136.2 16.2 %all_to_all.28 = f32[8,40,1,128]{3,1,2,0:T(8,128)S(1)} all-to-all(f32[8,40,1,128]{3,1,2,0:T(8,128)S(1)} %bitcast.30), channel_id=1, replica_groups=mesh['runs'=2,'far'=8,'near'=8,'core'=2] {'far'}, dimensions={0} | all-to-all | bytes 327680 | tf_op jit(solution)/shard_map/all_to_all | solution.py:351
  152.4 9.8 %all_to_all.29 = f32[8,40,1,128]{3,1,2,0:T(8,128)S(1)} all-to-all(f32[8,40,1,128]{3,1,2,0:T(8,128)S(1)} %bitcast.32), channel_id=1, replica_groups=mesh['runs'=2,'far'=8,'near'=8,'core'=2] {'near'}, dimensions={0} | all-to-all | bytes 327680 | tf_op jit(solution)/shard_map/all_to_all | solution.py:351
  162.2 4.4 %collective-permute-start.5 = (f32[320,128]{1,0:T(8,128)S(1)}, f32[320,128]{1,0:T(8,128)S(1)}, u32[]{:S(2)}, u32[]{:S(2)}) collective-permute-start(f32[320,128]{1,0:T(8,128)S(1)} %bitcast.26), channel_id=1, source_target_pairs={{0,1},{1,0},{2,3},{3,2},{4,5},{5,4},{6,7},{7,6},{8,9},{9,8},{10,11... | collective-permute-start | bytes 491528 | tf_op jit(solution)/shard_map/ppermute | solution.py:355
  166.6 1.0 collective-permute-done.5.other
  167.7 0.8 gather.1
  (3 shorter events, 0.1 us)
Async XLA Ops:
  68.2 11.4 %collective-permute-start = (f32[128,1024]{1,0:T(8,128)S(1)}, f32[128,1024]{1,0:T(8,128)S(1)}, u32[]{:S(2)}, u32[]{:S(2)}) collective-permute-start(f32[128,1024]{1,0:T(8,128)S(1)} %get-tuple-element.25.v), channel_id=1, source_target_pairs={{0,1},{1,0},{2,3},{3,2},{4,5},{5,4},{6,7},{7,6},{8,9},{9,8},{10,11... | collective-permute-start | bytes 1572872 | tf_op jit(solution)/shard_map/ppermute | solution.py:355
  68.8 7.9 %collective-permute-start.1 = (f32[64,1024]{1,0:T(8,128)S(1)}, f32[64,1024]{1,0:T(8,128)S(1)}, u32[]{:S(2)}, u32[]{:S(2)}) collective-permute-start(f32[64,1024]{1,0:T(8,128)S(1)} %get-tuple-element.26), channel_id=1, source_target_pairs={{0,2},{1,3},{2,0},{3,1},{4,6},{5,7},{6,4},{7,5},{8,10},{9,11},{10,... | collective-permute-start | bytes 786440 | tf_op jit(solution)/shard_map/ppermute | solution.py:355
  70.3 2.5 %copy-start = (f32[23]{0:T(128)S(1)}, f32[23]{0:T(128)}, u32[]{:S(2)}) copy-start(f32[23]{0:T(128)} %coef.3) | copy-start | bytes 280
  70.3 2.5 %copy-start.1 = (s32[23]{0:T(128)S(1)}, s32[23]{0:T(128)}, u32[]{:S(2)}) copy-start(s32[23]{0:T(128)} %mask.3) | copy-start | bytes 280
  70.3 8.4 %collective-permute-start.2 = (f32[64,1024]{1,0:T(8,128)S(1)}, f32[64,1024]{1,0:T(8,128)S(1)}, u32[]{:S(2)}, u32[]{:S(2)}) collective-permute-start(f32[64,1024]{1,0:T(8,128)S(1)} %get-tuple-element.27), channel_id=1, source_target_pairs={{0,6},{1,7},{2,4},{3,5},{4,2},{5,3},{6,0},{7,1},{8,14},{9,15},{10,... | collective-permute-start | bytes 786440 | tf_op jit(solution)/shard_map/ppermute | solution.py:355
  72.4 7.2 %collective-permute-start.3 = (f32[64,1024]{1,0:T(8,128)S(1)}, f32[64,1024]{1,0:T(8,128)S(1)}, u32[]{:S(2)}, u32[]{:S(2)}) collective-permute-start(f32[64,1024]{1,0:T(8,128)S(1)} %get-tuple-element.28), channel_id=1, source_target_pairs={{0,8},{1,9},{2,10},{3,11},{4,12},{5,13},{6,14},{7,15},{8,0},{9,1},... | collective-permute-start | bytes 786440 | tf_op jit(solution)/shard_map/ppermute | solution.py:355
  123.8 1.8 %collective-permute-start.4 = (f32[320,128]{1,0:T(8,128)S(1)}, f32[320,128]{1,0:T(8,128)S(1)}, u32[]{:S(2)}, u32[]{:S(2)}) collective-permute-start(f32[320,128]{1,0:T(8,128)S(1)} %get-tuple-element.42), channel_id=1, source_target_pairs={{0,1},{1,0},{2,3},{3,2},{4,5},{5,4},{6,7},{7,6},{8,9},{9,8},{10,11... | collective-permute-start | bytes 491528 | tf_op jit(solution)/shard_map/ppermute | solution.py:355
  162.2 5.4 %collective-permute-start.5 = (f32[320,128]{1,0:T(8,128)S(1)}, f32[320,128]{1,0:T(8,128)S(1)}, u32[]{:S(2)}, u32[]{:S(2)}) collective-permute-start(f32[320,128]{1,0:T(8,128)S(1)} %bitcast.26), channel_id=1, source_target_pairs={{0,1},{1,0},{2,3},{3,2},{4,5},{5,4},{6,7},{7,6},{8,9},{9,8},{10,11... | collective-permute-start | bytes 491528 | tf_op jit(solution)/shard_map/ppermute | solution.py:355

commit v6 on v5

--- a/solution.py
+++ b/solution.py
@@ -39,6 +39,11 @@
     rights = jnp.concatenate([right[0], right[1], right[0]], axis=right_dim)
     dims = (((left_dim,), (right_dim,)), ((), ()))
     return lax.dot_general(lefts, rights, dims, preferred_element_type=F32)
+
+
+def short_product(left, right):
+    dot = functools.partial(jnp.dot, preferred_element_type=F32)
+    return dot(left[0], right[0]) + (dot(left[0], right[1]) + dot(left[1], right[0]))
 
 
 def own_bits():
@@ -123,7 +128,7 @@
             for i in range(width):
                 left = (level_high[b, 2 * i], level_low[b, 2 * i])
                 right = (level_high[b, 2 * i + 1], level_low[b, 2 * i + 1])
-                high, low = halves(product(left, right, 1, 0))
+                high, low = halves(short_product(left, right))
                 if width > 1:
                     level_high[b, i], level_low[b, i] = high, low
                 else:
@@ -184,7 +189,8 @@
     return jnp.where(active & ((rows ^ columns) == ((1 << low) | (1 << high))), scale, 0.0)
 
 
-def local_hops_kernel(v, coef, mask, out):
+def local_hops_kernel(v, z, coef, mask, out, z_high, z_low):
+    z_high[...], z_low[...] = halves(z[...])
     lane_chain = sum(pair_matrix(LANE_BIT[k], LANE_BIT[k + 1], weight(coef, mask, k)) for k in range(6))
     top_chain = sum(pair_matrix(k, k + 1, weight(coef, mask, CHAIN_FIRST + k)) for k in range(6))
     lane_chain, top_chain = halves(lane_chain), halves(top_chain)
@@ -211,7 +217,9 @@
         out[:, c * LANES : (c + 1) * LANES] = total
 
 
-def return_kernel(hops, other, half4, half5, half6, coef, mask, u4_high, u4_low, z, gates, send, grams, lam, scratch):
+def return_kernel(
+    hops, other, half4, half5, half6, coef, mask, u4_high, u4_low, z_high, z_low, gates, send, grams, lam, scratch
+):
     bits = own_bits()
     lam[...] = hops[...]
     wide = lam.shape[1] // 2
@@ -234,10 +242,10 @@
         scratch[pl.ds(c, LANES, stride=LOW), :] = lam4[:, c * LANES : (c + 1) * LANES]
     g3 = gate(gates, 3)
     gram = jnp.zeros((LANES, LANES), F32)
-    for block in range(z.shape[0] // LANES):
+    for block in range(z_high.shape[0] // LANES):
         rows = slice(block * LANES, (block + 1) * LANES)
         inner = halves(scratch[rows, :])
-        gram = gram + product(inner, halves(z[rows, :]), 1, 1)
+        gram = gram + product(inner, (z_high[rows, :], z_low[rows, :]), 1, 1)
         send[rows, :] = product(g3, inner, 1, 0)
     grams[0] = gram
 
@@ -392,14 +400,20 @@
     )(z, gates)
     half4, half5, half6 = swapped(half4, 2), swapped(half5, 6), swapped(half6, 8)
     other = swapped(v, 1)
-    (hops,) = call(local_hops_kernel, [(turned, F32)], [VMEM, SMEM, SMEM], (), "hops")(v, hop_coef, hop_mask)
+    hops, z_high, z_low = call(
+        local_hops_kernel,
+        [(turned, F32), ((middle, LANES), BF16), ((middle, LANES), BF16)],
+        [VMEM, VMEM, SMEM, SMEM],
+        (),
+        "hops",
+    )(v, z, hop_coef, hop_mask)
     send, upper = call(
         return_kernel,
         [((middle, LANES), F32), ((2, LANES, LANES), F32)],
-        [VMEM] * 5 + [SMEM] * 2 + [VMEM] * 4,
+        [VMEM] * 5 + [SMEM] * 2 + [VMEM] * 5,
         [pltpu.VMEM(turned, F32), flat],
         "back",
-    )(hops, other, half4, half5, half6, hop_coef, hop_mask, u4_high, u4_low, z, gates)
+    )(hops, other, half4, half5, half6, hop_coef, hop_mask, u4_high, u4_low, z_high, z_low, gates)
     received = exchange(send, AMP)
     part = ((5 * LANES // CORES, LANES), F32)
     lam1_high, lam1_low, own, away = call(

time: 169 us -> 169 us (level)
  no operation moved by 1% of the time
where the time goes in v6:
time: 169 us; the launch traced here: 168 us
  blocking collectives  138 us (82%)
  Pallas kernels  13.8 us (8%)
  starting transfers between devices  9.7 us (6%)
  waiting for transfers between devices  5.76 us (3%)
    all_to_all x5, blocking collectives, exchange(): lax.all_to_all(shaped, axes, split_axis=0, concat_axis=0, tiled=True)  138 us
    pallas_call x10, Pallas kernels, run(): return made(*kept)  13.8 us
    ppermute x6, starting transfers between devices, swapped(): lax.ppermute(value, AMP, [(i, i ^ flip) for i in range(lax.axis_size(AMP))])  9.7 us
    ppermute x6, waiting for transfers between devices, swapped(): lax.ppermute(value, AMP, [(i, i ^ flip) for i in range(lax.axis_size(AMP))])  5.76 us
  transfers between devices with their start and end apart: 6, of which 4 were waited for; matrix products, arithmetic and copies ran while one was open for 0% of the time, Pallas kernels for 2%

profile of v6, /device:TPU:33, one launch (start us, length us, event | category | flops | bytes accessed | tf_op | source)
XLA Modules:
  0.0 168.3 jit_solution(15272743028798845979)
XLA Ops:
  0.6 5.1 %forward.1 = (f32[1024,128]{1,0:T(8,128)S(1)}, f32[1024,128]{1,0:T(8,128)S(1)}, bf16[256,512]{1,0:T(8,128)(2,1)S(1)}, bf16[256,512]{1,0:T(8,128)(2,1)S(1)}, bf16...) custom-call(f32[5,16]{1,0:T(8,128)} %angles_far.1, ...), custom_call_target="tpu_custom_call" | custom-call | tf_op jit(solution)/shard_map/forward/pallas_call | solution.py:351
  5.7 61.5 %all_to_all.25 = f32[128,8,1,128]{3,1,2,0:T(8,128)S(1)} all-to-all(f32[128,8,1,128]{3,1,2,0:T(8,128)S(1)} %bitcast.34), channel_id=1, replica_groups=mesh['runs'=2,'far'=8,'near'=8,'core'=2] {'far','near','core'}, dimensions={0} | all-to-all | bytes 1048576 | tf_op jit(solution)/shard_map/all_to_all | solution.py:359
  67.2 0.8 turn.1
  68.1 0.6 collective-permute-start
  68.7 1.5 collective-permute-start.1
  70.2 0.0 copy-start
  70.2 0.0 copy-start.1
  70.2 2.1 %collective-permute-start.2 = (f32[64,1024]{1,0:T(8,128)S(1)}, f32[64,1024]{1,0:T(8,128)S(1)}, u32[]{:S(2)}, u32[]{:S(2)}) collective-permute-start(f32[64,1024]{1,0:T(8,128)S(1)} %get-tuple-element.31), channel_id=1, source_target_pairs={{0,6},{1,7},{2,4},{3,5},{4,2},{5,3},{6,0},{7,1},{8,14},{9,15},{10,... | collective-permute-start | bytes 786440 | tf_op jit(solution)/shard_map/ppermute | solution.py:363
  72.3 0.5 collective-permute-start.3
  72.7 0.0 copy-done
  72.7 0.0 copy-done.1
  72.7 2.0 %hops.1 = (f32[128,1024]{1,0:T(8,128)S(1)}, bf16[1024,128]{1,0:T(8,128)(2,1)S(1)}, bf16[1024,128]{1,0:T(8,128)(2,1)S(1)}) custom-call(f32[128,1024]{1,0:T(8,128)S(1)} %get-tuple-element.28.v, f32[1024,128]{1,0:T(8,128)S(1)} %bitcast.24, f32[23]{0:T(128)S(1)} %copy-done, s32[23]{0:T(128)S(1)} %copy-done.1), custom_call_target="tpu_custom_call" | custom-call | tf_op jit(solution)/shard_map/hops/pallas_call | solution.py:351
  74.7 1.8 %collective-permute-done.1.half4 = f32[64,1024]{1,0:T(8,128)S(1)} collective-permute-done((f32[64,1024]{1,0:T(8,128)S(1)}, f32[64,1024]{1,0:T(8,128)S(1)}, u32[]{:S(2)}, u32[]{:S(2)}) %collective-permute-start.1) | collective-permute-done | bytes 262176 | tf_op jit(solution)/shard_map/ppermute | solution.py:363
  76.5 2.1 %collective-permute-done.2.half5 = f32[64,1024]{1,0:T(8,128)S(1)} collective-permute-done((f32[64,1024]{1,0:T(8,128)S(1)}, f32[64,1024]{1,0:T(8,128)S(1)}, u32[]{:S(2)}, u32[]{:S(2)}) %collective-permute-start.2) | collective-permute-done | bytes 262176 | tf_op jit(solution)/shard_map/ppermute | solution.py:363
  78.6 0.8 collective-permute-done.3.half6
  79.4 0.0 collective-permute-done.other
  79.4 2.0 %back.1 = (f32[1024,128]{1,0:T(8,128)S(1)}, f32[2,128,128]{2,1,0:T(8,128)S(1)}) custom-call(f32[128,1024]{1,0:T(8,128)S(1)} %get-tuple-element.29.hops, f32[128,1024]{1,0:T(8,128)S(1)} %collective-permute-done.other, f32[64,1024]{1,0:T(8,128)S(1)} %collective-permute-done.1.half4, f32[64,1024]{1,0:T(8,128)S(1)} %collective-permute-done.2.half5, ...), custom_call_target="tpu_custom_call" | custom-call | tf_op jit(solution)/shard_map/back/pallas_call | solution.py:351
  81.5 40.2 %all_to_all.26 = f32[128,8,1,128]{3,1,2,0:T(8,128)S(1)} all-to-all(f32[128,8,1,128]{3,1,2,0:T(8,128)S(1)} %bitcast.33), channel_id=1, replica_groups=mesh['runs'=2,'far'=8,'near'=8,'core'=2] {'far','near','core'}, dimensions={0} | all-to-all | bytes 1048576 | tf_op jit(solution)/shard_map/all_to_all | solution.py:359
  121.7 2.0 %backward.1 = (bf16[256,512]{1,0:T(8,128)(2,1)S(1)}, bf16[256,512]{1,0:T(8,128)(2,1)S(1)}, f32[320,128]{1,0:T(8,128)S(1)}, f32[320,128]{1,0:T(8,128)S(1)}) custom-call(f32[1024,128]{1,0:T(8,128)S(1)} %bitcast.25, f32[1024,128]{1,0:T(8,128)S(1)} %get-tuple-element.38.x, bf16[256,512]{1,0:T(8,128)(2,1)S(1)} %get-tuple-element.39.s1_high, ...), custom_call_target="tpu_custom_call" | custom-call | tf_op jit(solution)/shard_map/backward/pallas_call | solution.py:351
  123.7 0.6 collective-permute-start.4
  124.3 1.2 finish.1
  125.5 0.0 collective-permute-done.4.other
  125.5 10.6 %all_to_all.27 = f32[8,40,1,128]{3,1,2,0:T(8,128)S(1)} all-to-all(f32[8,40,1,128]{3,1,2,0:T(8,128)S(1)} %bitcast.28), channel_id=1, replica_groups=mesh['runs'=2,'far'=8,'near'=8,'core'=2] {'near'}, dimensions={0} | all-to-all | bytes 327680 | tf_op jit(solution)/shard_map/all_to_all | solution.py:359
  136.1 16.2 %all_to_all.28 = f32[8,40,1,128]{3,1,2,0:T(8,128)S(1)} all-to-all(f32[8,40,1,128]{3,1,2,0:T(8,128)S(1)} %bitcast.30), channel_id=1, replica_groups=mesh['runs'=2,'far'=8,'near'=8,'core'=2] {'far'}, dimensions={0} | all-to-all | bytes 327680 | tf_op jit(solution)/shard_map/all_to_all | solution.py:359
  152.3 9.8 %all_to_all.29 = f32[8,40,1,128]{3,1,2,0:T(8,128)S(1)} all-to-all(f32[8,40,1,128]{3,1,2,0:T(8,128)S(1)} %bitcast.32), channel_id=1, replica_groups=mesh['runs'=2,'far'=8,'near'=8,'core'=2] {'near'}, dimensions={0} | all-to-all | bytes 327680 | tf_op jit(solution)/shard_map/all_to_all | solution.py:359
  162.1 4.4 %collective-permute-start.5 = (f32[320,128]{1,0:T(8,128)S(1)}, f32[320,128]{1,0:T(8,128)S(1)}, u32[]{:S(2)}, u32[]{:S(2)}) collective-permute-start(f32[320,128]{1,0:T(8,128)S(1)} %bitcast.26), channel_id=1, source_target_pairs={{0,1},{1,0},{2,3},{3,2},{4,5},{5,4},{6,7},{7,6},{8,9},{9,8},{10,11... | collective-permute-start | bytes 491528 | tf_op jit(solution)/shard_map/ppermute | solution.py:363
  166.5 1.0 collective-permute-done.5.other
  167.6 0.8 gather.1
  (3 shorter events, 0.1 us)
Async XLA Ops:
  68.1 11.4 %collective-permute-start = (f32[128,1024]{1,0:T(8,128)S(1)}, f32[128,1024]{1,0:T(8,128)S(1)}, u32[]{:S(2)}, u32[]{:S(2)}) collective-permute-start(f32[128,1024]{1,0:T(8,128)S(1)} %get-tuple-element.28.v), channel_id=1, source_target_pairs={{0,1},{1,0},{2,3},{3,2},{4,5},{5,4},{6,7},{7,6},{8,9},{9,8},{10,11... | collective-permute-start | bytes 1572872 | tf_op jit(solution)/shard_map/ppermute | solution.py:363
  68.7 7.9 %collective-permute-start.1 = (f32[64,1024]{1,0:T(8,128)S(1)}, f32[64,1024]{1,0:T(8,128)S(1)}, u32[]{:S(2)}, u32[]{:S(2)}) collective-permute-start(f32[64,1024]{1,0:T(8,128)S(1)} %get-tuple-element.30), channel_id=1, source_target_pairs={{0,2},{1,3},{2,0},{3,1},{4,6},{5,7},{6,4},{7,5},{8,10},{9,11},{10,... | collective-permute-start | bytes 786440 | tf_op jit(solution)/shard_map/ppermute | solution.py:363
  70.2 2.5 %copy-start = (f32[23]{0:T(128)S(1)}, f32[23]{0:T(128)}, u32[]{:S(2)}) copy-start(f32[23]{0:T(128)} %coef.3) | copy-start | bytes 280
  70.2 2.5 %copy-start.1 = (s32[23]{0:T(128)S(1)}, s32[23]{0:T(128)}, u32[]{:S(2)}) copy-start(s32[23]{0:T(128)} %mask.3) | copy-start | bytes 280
  70.2 8.4 %collective-permute-start.2 = (f32[64,1024]{1,0:T(8,128)S(1)}, f32[64,1024]{1,0:T(8,128)S(1)}, u32[]{:S(2)}, u32[]{:S(2)}) collective-permute-start(f32[64,1024]{1,0:T(8,128)S(1)} %get-tuple-element.31), channel_id=1, source_target_pairs={{0,6},{1,7},{2,4},{3,5},{4,2},{5,3},{6,0},{7,1},{8,14},{9,15},{10,... | collective-permute-start | bytes 786440 | tf_op jit(solution)/shard_map/ppermute | solution.py:363
  72.3 7.2 %collective-permute-start.3 = (f32[64,1024]{1,0:T(8,128)S(1)}, f32[64,1024]{1,0:T(8,128)S(1)}, u32[]{:S(2)}, u32[]{:S(2)}) collective-permute-start(f32[64,1024]{1,0:T(8,128)S(1)} %get-tuple-element.32), channel_id=1, source_target_pairs={{0,8},{1,9},{2,10},{3,11},{4,12},{5,13},{6,14},{7,15},{8,0},{9,1},... | collective-permute-start | bytes 786440 | tf_op jit(solution)/shard_map/ppermute | solution.py:363
  123.7 1.8 %collective-permute-start.4 = (f32[320,128]{1,0:T(8,128)S(1)}, f32[320,128]{1,0:T(8,128)S(1)}, u32[]{:S(2)}, u32[]{:S(2)}) collective-permute-start(f32[320,128]{1,0:T(8,128)S(1)} %get-tuple-element.48), channel_id=1, source_target_pairs={{0,1},{1,0},{2,3},{3,2},{4,5},{5,4},{6,7},{7,6},{8,9},{9,8},{10,11... | collective-permute-start | bytes 491528 | tf_op jit(solution)/shard_map/ppermute | solution.py:363
  162.1 5.4 %collective-permute-start.5 = (f32[320,128]{1,0:T(8,128)S(1)}, f32[320,128]{1,0:T(8,128)S(1)}, u32[]{:S(2)}, u32[]{:S(2)}) collective-permute-start(f32[320,128]{1,0:T(8,128)S(1)} %bitcast.26), channel_id=1, source_target_pairs={{0,1},{1,0},{2,3},{3,2},{4,5},{5,4},{6,7},{7,6},{8,9},{9,8},{10,11... | collective-permute-start | bytes 491528 | tf_op jit(solution)/shard_map/ppermute | solution.py:363
